TPU v7x, 8 devices: a whole 2x2x1 slice. The times are simulated.
8 devices in a mesh: data: 1 (over z), img: 2 (over y), seq: 4 (over x, core).
Axes of the slice: x: 2, y: 2, z: 1, core: 2. Of those that a mesh axis runs over, the one named last changes fastest.
Arguments:
- x_in: bfloat16 [2, 16384, 384], P(('data', 'img'), 'seq')
- grad_y: bfloat16 [2, 16384, 384], P(('data', 'img'), 'seq')
- ln_gamma: float32 [384], replicated
- ln_beta: float32 [384], replicated
- w_qkv: bfloat16 [384, 1152], replicated
- w_out: bfloat16 [384, 384], replicated
- head_temp: float32 [8], replicated
Outputs:
- output 1: bfloat16 [2, 16384, 384], P(('data', 'img'), 'seq')
- output 2: bfloat16 [2, 16384, 384], P(('data', 'img'), 'seq')
- output 3: float32 [384, 1152], P(('data', 'seq'))
- output 4: float32 [384, 384], P(('data', 'seq'))
- output 5: float32 [384], P('data')
- output 6: float32 [384], P('data')
- output 7: float32 [8], P('data')
All inputs are finite; a program needn't handle non-finite values.
Results may differ from a plain program's by a relative error of at most 0.00418227.
Values are sent between devices in bfloat16 or wider.
A program may use at most 1 GiB of HBM per device.

v0:
```python
import jax
import jax.numpy as jnp
from jax import lax
from jax.sharding import PartitionSpec as P

LN_EPS = 1e-6


def layer_norm(x_f32, ln_gamma, ln_beta):
    row_mean = jnp.mean(x_f32, axis=-1, keepdims=True)
    centered = x_f32 - row_mean
    row_var = jnp.mean(centered * centered, axis=-1, keepdims=True)
    return centered * lax.rsqrt(row_var + LN_EPS) * ln_gamma + ln_beta


def attn_probs(gram_mat, sum_qq, sum_kk, head_temp):
    scale_mat = head_temp[..., :, None, None] * lax.rsqrt(sum_qq)[..., :, None] * lax.rsqrt(sum_kk)[..., None, :]
    return jax.nn.softmax(gram_mat * scale_mat, axis=-1)


def solution(mesh):
    act_spec = P(('data', 'img'), 'seq', None)
    row_spec = P(('data', 'seq'), None)
    in_specs = (act_spec, act_spec, P(), P(), P(), P(), P())
    out_specs = (act_spec, act_spec, row_spec, row_spec, P('data'), P('data'), P('data'))

    def local_block(x_in, grad_y, ln_gamma, ln_beta, w_qkv, w_out, head_temp):
        x_loc = x_in[0]
        gy_loc = grad_y[0]
        n_tok, model_dim = x_loc.shape
        n_heads = head_temp.shape[0]
        head_dim = model_dim // n_heads
        w_qkv4 = w_qkv.reshape(model_dim, 3, n_heads, head_dim)
        x_f32 = x_loc.astype(jnp.float32)
        u_f32, ln_pull = jax.vjp(layer_norm, x_f32, ln_gamma, ln_beta)
        u_act = u_f32.astype(jnp.bfloat16)
        qkv_all = jnp.einsum('nd,dchi->cnhi', u_act, w_qkv4, preferred_element_type=jnp.float32).astype(jnp.bfloat16)
        q_act = qkv_all[0]
        k_act = qkv_all[1]
        v_act = qkv_all[2]
        gram_part = jnp.einsum('nhi,nhj->hij', q_act, k_act, preferred_element_type=jnp.float32)
        sqq_part = jnp.sum(jnp.square(q_act.astype(jnp.float32)), axis=0)
        skk_part = jnp.sum(jnp.square(k_act.astype(jnp.float32)), axis=0)
        gram_mat, sum_qq, sum_kk = lax.psum((gram_part, sqq_part, skk_part), 'seq')
        attn_p, attn_pull = jax.vjp(attn_probs, gram_mat, sum_qq, sum_kk, head_temp)
        attn_pb = attn_p.astype(jnp.bfloat16)
        head_out = jnp.einsum('nhj,hij->nhi', v_act, attn_pb, preferred_element_type=jnp.float32).astype(jnp.bfloat16).reshape(n_tok, model_dim)
        proj_out = jnp.dot(head_out, w_out, preferred_element_type=jnp.float32)
        y_loc = (x_f32 + proj_out).astype(jnp.bfloat16)
        grad_o = jnp.einsum('ne,de->nd', gy_loc, w_out, preferred_element_type=jnp.float32).astype(jnp.bfloat16).reshape(n_tok, n_heads, head_dim)
        attn_part = jnp.einsum('nhi,nhj->hij', grad_o, v_act, preferred_element_type=jnp.float32)
        grad_attn = lax.psum(attn_part, 'seq')
        grad_v = jnp.einsum('nhi,hij->nhj', grad_o, attn_pb, preferred_element_type=jnp.float32)
        grad_gram, grad_sqq, grad_skk, grad_temp_img = attn_pull(grad_attn)
        gram_gb = grad_gram.astype(jnp.bfloat16)
        grad_q = jnp.einsum('nhj,hij->nhi', k_act, gram_gb, preferred_element_type=jnp.float32) + 2.0 * grad_sqq * q_act
        grad_k = jnp.einsum('nhi,hij->nhj', q_act, gram_gb, preferred_element_type=jnp.float32) + 2.0 * grad_skk * k_act
        grad_qkv = jnp.stack([grad_q, grad_k, grad_v]).astype(jnp.bfloat16)
        grad_u = jnp.einsum('cnhi,dchi->nd', grad_qkv, w_qkv4, preferred_element_type=jnp.float32).astype(jnp.bfloat16)
        grad_xln, gam_loc, bet_loc = ln_pull(grad_u.astype(jnp.float32))
        grad_x = (gy_loc.astype(jnp.float32) + grad_xln).astype(jnp.bfloat16)
        wqkv_loc = jnp.einsum('nd,cnhi->dchi', u_act, grad_qkv, preferred_element_type=jnp.float32).reshape(model_dim, 3 * model_dim)
        wout_loc = jnp.einsum('nd,ne->de', head_out, gy_loc, preferred_element_type=jnp.float32)
        grad_wqkv = lax.psum(lax.psum_scatter(wqkv_loc, 'seq', scatter_dimension=0, tiled=True), 'img')
        grad_wout = lax.psum(lax.psum_scatter(wout_loc, 'seq', scatter_dimension=0, tiled=True), 'img')
        grad_gamma, grad_beta = lax.psum((gam_loc, bet_loc), ('img', 'seq'))
        grad_temp = lax.psum(grad_temp_img, 'img')
        return y_loc[None], grad_x[None], grad_wqkv, grad_wout, grad_gamma, grad_beta, grad_temp

    return jax.shard_map(local_block, mesh=mesh, in_specs=in_specs, out_specs=out_specs, check_vma=False)
```

profile of v0, /device:TPU:0, one launch (start us, length us, event | category | flops | bytes accessed | tf_op | source)
XLA Modules:
  0.0 183.5 jit_solution(2451768047825779696)
XLA Ops:
  7.2 0.0 copy-start
  7.2 0.0 copy-start.2
  7.2 0.0 all-reduce.7.cloned.1.call-start
  7.3 0.0 copy-start.8
  7.3 2.7 %convert_reduce_fusion.1 = f32[4096]{0:T(1024)S(1)} fusion(bf16[1,4096,384]{2,1,0:T(8,128)(2,1)} %param.7), kind=kLoop, calls=%fused_computation.6 | loop fusion | flops 3141632 | bytes 3162112 | tf_op jit(solution)/shard_map/jvp()/reduce_sum | solution.py:10
  9.9 3.0 %fusion.14 = f32[4096]{0:T(1024)S(1)} fusion(bf16[1,4096,384]{2,1,0:T(8,128)(2,1)} %param.7, f32[4096]{0:T(1024)S(1)} %broadcast_multiply_fusion), kind=kLoop, calls=%fused_computation.27 | loop fusion | flops 6287360 | bytes 3178496 | tf_op jit(solution)/shard_map/jvp()/reduce_sum | solution.py:12
  13.0 5.4 %fusion.49 = f32[4096,1152]{0,1:S(1)} fusion(bf16[384,1152]{1,0:T(8,128)(2,1)S(1)} %copy-done.8, bf16[1,4096,384]{2,1,0:T(8,128)(2,1)S(1)} %copy-done.2, f32[384]{0:T(512)S(1)} %copy-done.11, f32[384]{0:T(512)S(1)} %copy-done.9, f32[4096]{0:T(1024)S(1)} %fusion.42, f32[4096]{0:T(1024)S(1)} %broadcast_multiply_fusion), kind=kOutput, calls=%fused_computation.83 | convolution fusion | flops 3633315840 | bytes 22940672
  18.4 1.4 convert_bitcast_fusion.1
  19.8 1.6 fusion.33
  21.4 2.6 %copy-done.3 = bf16[1,4096,384]{2,1,0:T(8,128)(2,1)S(1)} copy-done((bf16[1,4096,384]{2,1,0:T(8,128)(2,1)S(1)}, bf16[1,4096,384]{2,1,0:T(8,128)(2,1)}, u32[]{:S(2)}) %copy-start.3) | copy-done | bytes 3145752
  24.0 1.8 %convolution_convert_fusion.2 = bf16[4096,384]{0,1:T(8,128)(2,1)S(1)} fusion(bf16[384,384]{1,0:T(8,128)(2,1)S(1)} %copy-done, bf16[1,4096,384]{2,1,0:T(8,128)(2,1)S(1)} %copy-done.3), kind=kOutput, calls=%fused_computation.39 | convolution fusion | flops 1209532416 | bytes 6586368 | tf_op jit(solution)/shard_map/ne,de->nd/dot_general | solution.py:50
  25.9 1.6 copy-done.5
  27.5 2.0 %fusion.32 = f32[8,48,48]{2,1,0:T(8,128)} fusion(bf16[4096,8,48]{0,2,1:T(8,128)(2,1)S(1)} %bitcast.111, bf16[3,4096,8,48]{1,3,2,0:T(8,128)(2,1)S(1)} %convert_bitcast_fusion.1), kind=kOutput, calls=%fused_computation.53 | convolution fusion | flops 150994944 | bytes 6365184 | tf_op jit(solution)/shard_map/nhi,nhj->hij/dot_general | solution.py:51
  29.5 0.0 all-reduce.7.cloned.1.call-update
  29.5 0.0 reduce-scatter.5.cloned.1.call-start
  29.6 3.5 %fusion.8 = (f32[8,48]{1,0:T(8,128)S(1)}, f32[8,48]{1,0:T(8,128)S(1)}) fusion(bf16[3,4096,8,48]{1,3,2,0:T(8,128)(2,1)} %copy-done.1), kind=kLoop, calls=%fused_computation.21 | loop fusion | flops 9436416 | bytes 6294528 | tf_op jit(solution)/shard_map/reduce_sum | solution.py:42
  33.1 9.1 %all-reduce.1 = (f32[8,48]{1,0:T(8,128)S(1)}, f32[8,48]{1,0:T(8,128)S(1)}) all-reduce(f32[8,48]{1,0:T(8,128)S(1)} %get-tuple-element.8, f32[8,48]{1,0:T(8,128)S(1)} %get-tuple-element.7), channel_id=1, replica_groups=mesh['data'=1,'img'=2,'seq'=4] {'seq'}, use_global_device_ids=true, to_apply=%region_6.0 | all-reduce | flops 768 | bytes 6144 | tf_op jit(solution)/shard_map/psum | solution.py:44
  42.2 0.1 rsqrt_multiply_fusion.1
  42.3 2.2 %copy.18 = bf16[384,1152]{0,1:T(8,128)(2,1)} copy(bf16[384,1152]{1,0:T(8,128)(2,1)} %param.11) | data formatting | bytes 1769472 | tf_op args[4]
  44.5 15.2 %all-reduce.7.cloned.1.call-done = (f32[8,48,48]{2,1,0:T(8,128)}, f32[8,48,48]{2,1,0:T(8,128)}) async-done(((f32[8,48,48]{2,1,0:T(8,128)}, f32[8,48,48]{2,1,0:T(8,128)}), (f32[8,48,48]{2,1,0:T(8,128)}, f32[8,48,48]{2,1,0:T(8,128)})) %all-reduce.7.cloned.1.call-update) | async-done | bytes 147472 | tf_op jit(solution)/shard_map/psum | solution.py:44
  59.8 2.0 %fusion.51 = (f32[8,48]{1,0:T(8,128)S(1)}, f32[8,48,48]{2,1,0:T(8,128)}) fusion(f32[8,48,48]{2,1,0:T(8,128)} %get-tuple-element.19, f32[8,48]{1,0:T(8,128)S(1)} %rsqrt.18, f32[8,48]{1,0:T(8,128)S(1)} %rsqrt_multiply_fusion.1), kind=kOutput, calls=%fused_computation.84 | output fusion | flops 73775 | bytes 152064 | tf_op jit(solution)/shard_map/jvp()/sub | solution.py:18
  61.8 5.4 %convolution_convert_fusion.1 = bf16[8,48,4096]{2,1,0:T(8,128)(2,1)} fusion(bf16[3,4096,8,48]{1,3,2,0:T(8,128)(2,1)} %copy-done.1, f32[8,48]{1,0:T(8,128)S(1)} %get-tuple-element.26, f32[8,48,48]{2,1,0:T(8,128)} %get-tuple-element.19, f32[8,48]{1,0:T(8,128)S(1)} %rsqrt.18, f32[8,48]{1,0:T(8,128)S(1)} %rsqrt_multiply_fusion.1), kind=kOutput, calls=%fused_computation.38 | convolution fusion | flops 152660400 | bytes 6492672 | tf_op jit(solution)/shard_map/nhj,hij->nhi/dot_general | solution.py:47
  67.1 5.2 %fusion.22 = bf16[1,4096,8,48]{1,3,2,0:T(8,128)(2,1)} fusion(bf16[4096,8,48]{0,2,1:T(8,128)(2,1)} %bitcast.112, f32[8,48]{1,0:T(8,128)S(1)} %get-tuple-element.26, f32[8,48,48]{2,1,0:T(8,128)} %get-tuple-element.19, f32[8,48]{1,0:T(8,128)S(1)} %rsqrt.18, f32[8,48]{1,0:T(8,128)S(1)} %rsqrt_multiply_fusion.1), kind=kOutput, calls=%fused_computation.40 | convolution fusion | flops 152660400 | bytes 6369792 | tf_op jit(solution)/shard_map/nhi,hij->nhj/dot_general | solution.py:53
  72.3 1.3 multiply_reduce_fusion.2
  73.6 1.4 multiply_reduce_fusion.1
  75.0 0.1 fusion.46
  75.2 6.0 %fusion.24 = bf16[1,4096,8,48]{1,3,2,0:T(8,128)(2,1)} fusion(f32[8,48]{1,0:T(8,128)S(1)} %multiply_multiply_fusion.4, bf16[3,4096,8,48]{1,3,2,0:T(8,128)(2,1)} %copy-done.1, f32[8,48,48]{2,1,0:T(8,128)S(1)} %get-tuple-element.23, f32[8,48]{1,0:T(8,128)S(1)} %rsqrt.18, f32[8,48]{1,0:T(8,128)S(1)} %rsqrt_multiply_fusion.1), kind=kOutput, calls=%fused_computation.42 | convolution fusion | flops 157341696 | bytes 9515520 | tf_op jit(solution)/shard_map/nhi,hij->nhj/dot_general | solution.py:57
  81.2 5.8 %fusion.25 = bf16[1,4096,8,48]{1,3,2,0:T(8,128)(2,1)} fusion(f32[8,48]{1,0:T(8,128)S(1)} %get-tuple-element.25, bf16[3,4096,8,48]{1,3,2,0:T(8,128)(2,1)} %copy-done.1, f32[8,48,48]{2,1,0:T(8,128)S(1)} %get-tuple-element.23, f32[8,48]{1,0:T(8,128)S(1)} %rsqrt.18, f32[8,48]{1,0:T(8,128)S(1)} %rsqrt_multiply_fusion.1), kind=kOutput, calls=%fused_computation.43 | convolution fusion | flops 157341696 | bytes 9515520 | tf_op jit(solution)/shard_map/nhj,hij->nhi/dot_general | solution.py:56
  87.0 2.6 %fusion.29 = f32[384,384]{1,0:T(8,128)} fusion(bf16[4096,384]{0,1:T(8,128)(2,1)S(1)} %bitcast.115, bf16[1,4096,384]{2,1,0:T(8,128)(2,1)S(1)} %copy-done.4), kind=kOutput, calls=%fused_computation.50 | convolution fusion | flops 1207959552 | bytes 6881280 | tf_op jit(solution)/shard_map/nd,ne->de/dot_general | solution.py:63
  89.6 0.0 reduce-scatter.5.cloned.1.call-update
  89.7 0.3 reduce-scatter.3.cloned.1.call-start
  89.9 8.4 %pad_maximum_fusion = bf16[3,4096,8,48]{1,3,2,0:T(8,128)(2,1)} fusion(bf16[1,4096,8,48]{1,3,2,0:T(8,128)(2,1)} %fusion.22, bf16[1,4096,8,48]{1,3,2,0:T(8,128)(2,1)} %fusion.24, bf16[1,4096,8,48]{1,3,2,0:T(8,128)(2,1)} %fusion.25), kind=kLoop, calls=%fused_computation.8 | loop fusion | flops 9437184 | bytes 18874368 | tf_op jit(solution)/shard_map/stack | solution.py:58
  98.3 10.4 %fusion.47 = f32[384,1152]{1,0:T(8,128)} fusion(bf16[1152,4096]{1,0:T(8,128)(2,1)} %bitcast.113, bf16[1,4096,384]{2,1,0:T(8,128)(2,1)S(1)} %copy-done.2, f32[384]{0:T(512)S(1)} %copy-done.11, f32[384]{0:T(512)S(1)} %copy-done.9, f32[4096]{0:T(1024)S(1)} %fusion.42, f32[4096]{0:T(1024)S(1)} %broadcast_multiply_fusion), kind=kOutput, calls=%fused_computation.82 | convolution fusion | flops 3633315840 | bytes 14388224 | tf_op jit(solution)/shard_map/nd,cnhi->dchi/dot_general | solution.py:62
  108.7 0.0 reduce-scatter.3.cloned.1.call-update
  108.7 0.0 all-reduce.9.cloned.1.call-start
  108.7 9.7 %convert_reduce_fusion = (f32[384]{0:T(512)S(1)}, f32[4096]{0:T(1024)S(1)}, bf16[4096,384]{1,0:T(8,128)(2,1)S(1)}) fusion(f32[384]{0:T(512)S(1)} %copy-done.9, f32[4096]{0:T(1024)S(1)} %broadcast_multiply_fusion, bf16[1,4096,384]{2,1,0:T(8,128)(2,1)S(1)} %copy-done.2, bf16[384,3,8,48]{0,3,2,1:T(8,128)(2,1)} %bitcast.116, ...), kind=kOutput, calls=%fused_computation.2 | convolution fusion | flops 3645894144 | bytes 16649216 | tf_op jit(solution)/shard_map/cnhi,dchi->nd/dot_general | solution.py:59
  118.5 0.0 copy-start.6
  118.5 1.6 copy-done.6
  120.2 3.5 %fusion.21 = (f32[384]{0:T(512)S(1)}, f32[4096]{0:T(1024)S(1)}) fusion(bf16[4096,384]{1,0:T(8,128)(2,1)S(1)} %get-tuple-element.28, bf16[1,4096,384]{2,1,0:T(8,128)(2,1)S(1)} %copy-done.2, f32[4096]{0:T(1024)S(1)} %fusion.42, f32[4096]{0:T(1024)S(1)} %broadcast_multiply_fusion, f32[4096]{0:T(1024)S(1)} %multiply_multiply_fusion.3, f32[384]{0:T(512)S(1)} %copy-done.9), kind=kLoop, calls=%fused_computation.34 | loop fusion | flops 18869888 | bytes 6360064 | tf_op jit(solution)/shard_map/transpose(jvp())/reduce_sum | solution.py:13
  123.7 0.0 reduce-scatter.5.cloned.1.call-done
  123.7 8.7 %reduce-scatter.3.cloned.1.call-done = f32[96,1152]{1,0:T(8,128)} async-done(((f32[384,1152]{1,0:T(8,128)}), f32[96,1152]{1,0:T(8,128)}) %reduce-scatter.3.cloned.1.call-update) | async-done | bytes 442384 | tf_op jit(solution)/shard_map/reduce_scatter | solution.py:64
  132.4 0.0 all-reduce.9.cloned.1.call-update
  132.4 7.3 %fusion.27 = bf16[1,4096,384]{2,1,0:T(8,128)(2,1)} fusion(bf16[1,4096,384]{2,1,0:T(8,128)(2,1)S(1)} %copy-done.2, bf16[4096,384]{1,0:T(8,128)(2,1)} %copy-done.6, bf16[1,4096,384]{2,1,0:T(8,128)(2,1)} %param.8, f32[4096]{0:T(1024)S(1)} %negate_multiply_fusion, f32[4096]{0:T(1024)S(1)} %multiply_multiply_fusion.3, f32[4096]{0:T(1024)S(1)} %fusion.42, ...), kind=kLoop, calls=%fused_computation.45 | loop fusion | flops 18874368 | bytes 12649984 | tf_op jit(solution)/shard_map/broadcast_in_dim | solution.py:68
  139.7 5.5 %psum.71 = f32[8]{0:T(128)} all-reduce(f32[8]{0:T(128)S(1)} %get-tuple-element.24), channel_id=1, replica_groups=mesh['data'=1,'img'=2,'seq'=4] {'img'}, use_global_device_ids=true, to_apply=%region_24.0 | all-reduce | flops 8 | bytes 64 | tf_op jit(solution)/shard_map/psum | solution.py:67
  145.2 22.6 %all-reduce = (f32[384]{0:T(512)}, f32[384]{0:T(512)}) all-reduce(f32[384]{0:T(512)S(1)} %get-tuple-element.9, f32[384]{0:T(512)S(1)} %get-tuple-element.11), channel_id=1, replica_groups=mesh['data'=1,'img'=2,'seq'=4] {'img','seq'}, use_global_device_ids=true, to_apply=%region_20.0 | all-reduce | flops 768 | bytes 6144 | tf_op jit(solution)/shard_map/psum | solution.py:66
  167.9 5.7 %fusion.23 = bf16[1,4096,384]{2,1,0:T(8,128)(2,1)} fusion(bf16[4096,384]{0,1:T(8,128)(2,1)} %bitcast.114, bf16[384,384]{1,0:T(8,128)(2,1)S(1)} %copy-done, bf16[1,4096,384]{2,1,0:T(8,128)(2,1)S(1)} %copy-done.2), kind=kOutput, calls=%fused_computation.41 | convolution fusion | flops 1212678144 | bytes 9732096 | tf_op jit(solution)/shard_map/dot_general | solution.py:48
  173.6 1.8 copy.28
  175.4 1.6 copy.29
  (26 shorter events, 0.1 us)
Async XLA Ops:
  7.2 14.3 %copy-start = (bf16[384,384]{1,0:T(8,128)(2,1)S(1)}, bf16[384,384]{1,0:T(8,128)(2,1)}, u32[]{:S(2)}) copy-start(bf16[384,384]{1,0:T(8,128)(2,1)} %param.12) | copy-start | bytes 884740
  7.2 5.8 %copy-start.2 = (bf16[1,4096,384]{2,1,0:T(8,128)(2,1)S(1)}, bf16[1,4096,384]{2,1,0:T(8,128)(2,1)}, u32[]{:S(2)}) copy-start(bf16[1,4096,384]{2,1,0:T(8,128)(2,1)} %param.7) | copy-start | bytes 9437188
  7.2 5.8 %copy-start.11 = (f32[384]{0:T(512)S(1)}, f32[384]{0:T(512)}, u32[]{:S(2)}) copy-start(f32[384]{0:T(512)} %param.10) | copy-start | bytes 4612
  7.2 5.8 %copy-start.9 = (f32[384]{0:T(512)S(1)}, f32[384]{0:T(512)}, u32[]{:S(2)}) copy-start(f32[384]{0:T(512)} %param.9) | copy-start | bytes 4612
  7.2 52.5 %all-reduce.7.cloned.1.call-start = ((), (), s32[]{:S(2)}) async-start(), calls=%async_computation.4 | async-start | bytes 786432 | tf_op jit(solution)/shard_map/psum | solution.py:44
  7.3 5.8 %copy-start.8 = (bf16[384,1152]{1,0:T(8,128)(2,1)S(1)}, bf16[384,1152]{1,0:T(8,128)(2,1)}, u32[]{:S(2)}) copy-start(bf16[384,1152]{1,0:T(8,128)(2,1)} %param.11) | copy-start | bytes 2654212
  19.8 6.1 %copy-start.1 = (bf16[3,4096,8,48]{1,3,2,0:T(8,128)(2,1)}, bf16[3,4096,8,48]{1,3,2,0:T(8,128)(2,1)S(1)}, u32[]{:S(2)}) copy-start(bf16[3,4096,8,48]{1,3,2,0:T(8,128)(2,1)S(1)} %convert_bitcast_fusion.1) | copy-start | bytes 28311556
  19.8 4.2 %copy-start.3 = (bf16[1,4096,384]{2,1,0:T(8,128)(2,1)S(1)}, bf16[1,4096,384]{2,1,0:T(8,128)(2,1)}, u32[]{:S(2)}) copy-start(bf16[1,4096,384]{2,1,0:T(8,128)(2,1)} %param.8) | copy-start | bytes 9437188
  25.9 1.7 copy-start.5
  27.5 14.7 %copy-start.10 = (f32[8]{0:T(128)S(1)}, f32[8]{0:T(128)}, u32[]{:S(2)}) copy-start(f32[8]{0:T(128)} %param.13) | copy-start | bytes 100
  29.5 94.2 %reduce-scatter.5.cloned.1.call-start = ((), (), s32[]{:S(2)}) async-start(), calls=%async_computation.3 | async-start | bytes 737280 | tf_op jit(solution)/shard_map/reduce_scatter | solution.py:65
  75.2 11.8 %copy-start.4 = (bf16[1,4096,384]{2,1,0:T(8,128)(2,1)S(1)}, bf16[1,4096,384]{2,1,0:T(8,128)(2,1)}, u32[]{:S(2)}) copy-start(bf16[1,4096,384]{2,1,0:T(8,128)(2,1)} %param.8) | copy-start | bytes 9437188
  75.2 11.8 %copy-start.7 = (bf16[8,48,4096]{2,1,0:T(8,128)(2,1)S(1)}, bf16[8,48,4096]{2,1,0:T(8,128)(2,1)}, u32[]{:S(2)}) copy-start(bf16[8,48,4096]{2,1,0:T(8,128)(2,1)} %convolution_convert_fusion.1) | copy-start | bytes 9437188
  89.7 42.7 %reduce-scatter.3.cloned.1.call-start = ((), (), s32[]{:S(2)}) async-start(), calls=%async_computation.2 | async-start | bytes 2211840 | tf_op jit(solution)/shard_map/reduce_scatter | solution.py:64
  108.7 64.9 %all-reduce.9.cloned.1.call-start = ((), (), s32[]{:S(2)}) async-start(), calls=%async_computation.5 | async-start | bytes 1179648 | tf_op jit(solution)/shard_map/psum | solution.py:64
  118.5 1.7 copy-start.6
Sparse Core Ops, SparseCore 0:
  29.6 30.0 all-reduce.6
  89.8 16.3 reduce-scatter.4
  108.8 23.5 reduce-scatter.2
  134.6 24.5 all-reduce.8
where the time goes:
time: 184 us; the launch traced here: 183 us
  matrix products  61.6 us (33%)
  blocking collectives  37.2 us (20%)
  other arithmetic  34.7 us (19%)
  waiting for transfers between devices  24 us (13%)
  between operations  14 us (8%)
  local copies, waits for them, and re-layouts  11.5 us (6%)
    psum x1, blocking collectives, local_block(): grad_gamma, grad_beta = lax.psum((gam_loc, bet_loc), ('img', 'seq'))  22.6 us
    psum x1, waiting for transfers between devices, local_block(): gram_mat, sum_qq, sum_kk = lax.psum((gram_part, sqq_part, skk_part), 'seq')  15.2 us
    unnamed x27, local copies, waits for them, and re-layouts  11.5 us
    dot_general x1, matrix products, local_block(): jnp.einsum('nd,cnhi->dchi', u_act, grad_qkv, preferred_element_type=jnp.f...  10.4 us
    dot_general x1, matrix products, local_block(): jnp.einsum('cnhi,dchi->nd', grad_qkv, w_qkv4, preferred_element_type=jnp....  9.74 us
    psum x1, blocking collectives, local_block(): gram_mat, sum_qq, sum_kk = lax.psum((gram_part, sqq_part, skk_part), 'seq')  9.11 us
    reduce_scatter x1, waiting for transfers between devices, local_block(): lax.psum_scatter(wqkv_loc, 'seq', scatter_dimension=0, tiled=True)  8.68 us
    another operation x1, other arithmetic, local_block(): grad_qkv = jnp.stack([grad_q, grad_k, grad_v]).astype(jnp.bfloat16)  8.39 us
  transfers between devices with their start and end apart: 4, of which 2 were waited for; matrix products, arithmetic and copies ran while one was open for 28% of the time, Pallas kernels for 0%

commit v1 on v0

v1 whole, which is shorter than its diff:
```python
import functools

import jax
import jax.numpy as jnp
from jax import lax
from jax.experimental import pallas as pl
from jax.experimental.pallas import tpu as pltpu
from jax.sharding import PartitionSpec as P

LN_EPS = 1e-6
MESH = pl.DeviceIdType.MESH
F32 = jnp.float32
BF16 = jnp.bfloat16

D = 384
H = 8
C = 48
SPLIT = 240
OFF = 128
ROWS = 96
TB = 512


def mm(a, b):
    return jnp.dot(a, b, preferred_element_type=F32)


def mm_nt(a, b):
    return lax.dot_general(a, b, (((1,), (1,)), ((), ())), preferred_element_type=F32)


def col_mask(h):
    col = lax.broadcasted_iota(jnp.int32, (C, D), 1)
    return (col >= C * h) & (col < C * h + C)


def to_column(row, h):
    col = lax.broadcasted_iota(jnp.int32, (C, D), 1)
    line = lax.broadcasted_iota(jnp.int32, (C, D), 0)
    return jnp.sum(jnp.where(col == line + C * h, row, 0.0), axis=1, keepdims=True)


def to_row(column, h):
    col = lax.broadcasted_iota(jnp.int32, (C, D), 1)
    line = lax.broadcasted_iota(jnp.int32, (C, D), 0)
    return jnp.sum(jnp.where(col == line + C * h, column, 0.0), axis=0, keepdims=True)


def pack(lo, hi):
    p_lo = jnp.zeros((C, 256), F32)
    p_hi = jnp.zeros((C, 256), F32)
    for h in range(5):
        p_lo += jnp.where(col_mask(h)[:, 0:256], lo[C * h : C * h + C, :], 0.0)
    for h in range(5, H):
        r = C * h - SPLIT
        p_hi += jnp.where(col_mask(h)[:, OFF:D], hi[r : r + C, :], 0.0)
    return jnp.concatenate([p_lo[:, 0:128], p_lo[:, 128:256] + p_hi[:, 0:128], p_hi[:, 128:256]], axis=1)


def block_mm(w, act):
    lo = mm(w[0:SPLIT, 0:256], act[0:256, :])
    hi = mm(w[SPLIT:D, OFF:D], act[OFF:D, :])
    return lo, hi


def kernel(
    nb,
    x_hbm, dy_hbm, gamma_ref, beta_ref, wqkv_ref, wo_ref, tau_ref,
    y_hbm, dx_hbm, gwqkv_ref, gwo_ref, ggam_ref, gbet_ref, gtau_ref,
    x_v, dy_v, y_v, ut, qkvt, dot_v, ot, mean_v, rstd_v, wqkvt,
    g_lo, g_hi, sq_acc, sk_acc, ex_g, ex_a, a_f, a_b, a_bt, dg_b, dg_bt, dsq_v, dsk_v,
    pw, ra, sa, rb, sb, rc, gb_acc, ex_gb, ex_t,
    x_sem, dy_sem, y_sem, dx_sem,
    exg_s, exg_r, exa_s, exa_r, a_s, a_r, b_s, b_r, c_s, c_r, gb_s, gb_r, t_s, t_r,
):
    data = lax.axis_index("data")
    img = lax.axis_index("img")
    seq = lax.axis_index("seq")
    xc = seq // 2
    core = seq % 2

    def dev(k):
        i = 1 - img if k & 4 else img
        xx = 1 - xc if k & 2 else xc
        cc = 1 - core if k & 1 else core
        return (data, i, xx * 2 + cc)

    barrier = pltpu.get_barrier_semaphore()
    for k in range(1, 8):
        pl.semaphore_signal(barrier, inc=1, device_id=dev(k), device_id_type=MESH)

    def x_in(t):
        return pltpu.make_async_copy(x_hbm.at[t], x_v.at[t], x_sem.at[t])

    def dy_in(t):
        return pltpu.make_async_copy(dy_hbm.at[t], dy_v.at[t], dy_sem.at[t])

    def y_out(t):
        return pltpu.make_async_copy(y_v.at[t], y_hbm.at[t], y_sem.at[t])

    def dx_out(t):
        return pltpu.make_async_copy(dy_v.at[t], dx_hbm.at[t], dx_sem.at[t])

    for t in range(nb):
        x_in(t).start()
    for t in range(nb):
        dy_in(t).start()

    def remote(src, dst, s, r, k):
        return pltpu.make_async_remote_copy(
            src_ref=src, dst_ref=dst, send_sem=s, recv_sem=r, device_id=dev(k), device_id_type=MESH
        )

    def small(buf, s, r, k):
        return remote(buf.at[0], buf.at[k], s.at[k], r.at[k], k)

    def stage_a(c, xx):
        rows = pl.ds(pl.multiple_of(ROWS * (2 * xx + 1 - core), 8), ROWS)
        return remote(pw.at[c, rows, :], ra.at[c, xx], a_s.at[c, xx], a_r.at[c, xx], 1)

    def stage_b(c):
        return remote(sa.at[c, 1 - xc], rb.at[c], b_s.at[c], b_r.at[c], 2)

    def stage_c(c):
        return remote(sb.at[c], rc.at[c], c_s.at[c], c_r.at[c], 4)

    def start_a(c):
        for xx in range(2):
            stage_a(c, xx).start()

    def start_b(c):
        for xx in range(2):
            stage_a(c, xx).wait_recv()
            rows = pl.ds(pl.multiple_of(ROWS * (2 * xx + core), 8), ROWS)
            sa[c, xx] = pw[c, rows, :] + ra[c, xx]
        stage_b(c).start()

    def start_c(c):
        stage_b(c).wait_recv()
        sb[c] = sa[c, xc] + rb[c]
        stage_c(c).start()

    wqkvt[...] = wqkv_ref[...].T
    for ref in (g_lo, g_hi, sq_acc, sk_acc, gb_acc, pw):
        ref[...] = jnp.zeros_like(ref)
    gamma = gamma_ref[...]
    beta = beta_ref[...]

    def lane_fold(a):
        out = a[:, 0:128]
        for i in range(1, TB // 128):
            out = out + a[:, 128 * i : 128 * i + 128]
        return out

    def phase1(t, carry):
        x_in(t).wait()
        x = x_v[t].astype(F32)
        mean = jnp.mean(x, axis=-1, keepdims=True)
        cen = x - mean
        var = jnp.mean(cen * cen, axis=-1, keepdims=True)
        rstd = lax.rsqrt(var + LN_EPS)
        mean_v[t] = jnp.broadcast_to(mean, (TB, 128))
        rstd_v[t] = jnp.broadcast_to(rstd, (TB, 128))
        u = (cen * rstd * gamma + beta).astype(BF16)
        u_t = u.T
        ut[t] = u_t
        qk = mm(wqkvt[0 : 2 * D, :], u_t).astype(BF16)
        qkvt[t, 0 : 2 * D, :] = qk
        q = qk[0:D, :]
        k = qk[D : 2 * D, :]
        g_lo[...] += mm_nt(q[0:SPLIT, :], k[0:256, :])
        g_hi[...] += mm_nt(q[SPLIT:D, :], k[OFF:D, :])
        qf = q.astype(F32)
        kf = k.astype(F32)
        sq_acc[...] += lane_fold(qf * qf)
        sk_acc[...] += lane_fold(kf * kf)
        return carry

    lax.fori_loop(0, nb, phase1, 0)

    ex_g[0, 0:C, :] = pack(g_lo[...], g_hi[...])
    sq_row = jnp.zeros((1, D), F32)
    sk_row = jnp.zeros((1, D), F32)
    for h in range(H):
        rows = slice(C * h, C * h + C)
        sq_row += to_row(jnp.sum(sq_acc[rows, :], axis=1, keepdims=True), h)
        sk_row += to_row(jnp.sum(sk_acc[rows, :], axis=1, keepdims=True), h)
    ex_g[0, C : C + 8, :] = jnp.concatenate([sq_row, sk_row, jnp.zeros((6, D), F32)], axis=0)
    pl.semaphore_wait(barrier, 7)
    for k in range(1, 4):
        small(ex_g, exg_s, exg_r, k).start()

    g_lo[...] = jnp.zeros_like(g_lo)
    g_hi[...] = jnp.zeros_like(g_hi)

    def phase2(t, carry):
        dy_in(t).wait()
        v = mm(wqkvt[2 * D : 3 * D, :], ut[t]).astype(BF16)
        qkvt[t, 2 * D : 3 * D, :] = v
        do = mm_nt(wo_ref[...], dy_v[t]).astype(BF16)
        dot_v[t] = do
        g_lo[...] += mm_nt(do[0:SPLIT, :], v[0:256, :])
        g_hi[...] += mm_nt(do[SPLIT:D, :], v[OFF:D, :])
        return carry

    lax.fori_loop(0, nb, phase2, 0)
    ex_a[0] = pack(g_lo[...], g_hi[...])
    for k in range(1, 4):
        small(ex_a, exa_s, exa_r, k).start()

    for k in range(1, 4):
        small(ex_g, exg_s, exg_r, k).wait_recv()
    gram_all = (ex_g[0] + ex_g[1]) + (ex_g[2] + ex_g[3])
    gram = gram_all[0:C, :]
    sq_row = gram_all[C : C + 1, :]
    sk_row = gram_all[C + 1 : C + 2, :]
    rk = lax.rsqrt(sk_row)
    for h in range(H):
        m = col_mask(h)
        rq = lax.rsqrt(to_column(sq_row, h))
        z = jnp.where(m, gram * (tau_ref[h] * rq * rk), -jnp.inf)
        e = jnp.exp(z - jnp.max(z, axis=1, keepdims=True))
        a = e / jnp.sum(e, axis=1, keepdims=True)
        a_f[h] = a
        a_b[C * h : C * h + C, :] = a.astype(BF16)
    a_bt[...] = a_b[...].T

    def phase3(t, carry):
        o_lo, o_hi = block_mm(a_b[...], qkvt[t, 2 * D : 3 * D, :])
        ot[t, 0:SPLIT, :] = o_lo.astype(BF16)
        ot[t, SPLIT:D, :] = o_hi.astype(BF16)
        pw[0] += mm(ot[t], dy_v[t])
        return carry

    lax.fori_loop(0, nb, phase3, 0)
    start_a(0)

    def phase4(t, carry):
        dv_lo, dv_hi = block_mm(a_bt[...], dot_v[t])
        qkvt[t, 2 * D : 2 * D + SPLIT, :] = dv_lo.astype(BF16)
        qkvt[t, 2 * D + SPLIT : 3 * D, :] = dv_hi.astype(BF16)
        pw[1] += mm_nt(ut[t], qkvt[t, 2 * D : 3 * D, :])

        @pl.when(t == 3)
        def _():
            start_b(0)

        return carry

    lax.fori_loop(0, nb, phase4, 0)
    start_a(1)

    for k in range(1, 4):
        small(ex_a, exa_s, exa_r, k).wait_recv()
    d_attn = (ex_a[0] + ex_a[1]) + (ex_a[2] + ex_a[3])
    drk = jnp.zeros((1, D), F32)
    lane = lax.broadcasted_iota(jnp.int32, (8, 128), 1)
    dtau = jnp.zeros((8, 128), F32)
    for h in range(H):
        m = col_mask(h)
        tau = tau_ref[h]
        sq = to_column(sq_row, h)
        rq = lax.rsqrt(sq)
        a = a_f[h]
        da = jnp.where(m, d_attn, 0.0)
        dz = a * (da - jnp.sum(da * a, axis=1, keepdims=True))
        dg_b[C * h : C * h + C, :] = jnp.where(m, dz * (tau * rq * rk), 0.0).astype(BF16)
        w = dz * gram
        wrk = jnp.sum(jnp.where(m, w * rk, 0.0), axis=1, keepdims=True)
        dsq = (tau * wrk) * (-0.5 * (rq / sq))
        dsq_v[C * h : C * h + C, :] = jnp.broadcast_to(2.0 * dsq, (C, 128))
        drk += jnp.sum(jnp.where(m, w * (tau * rq), 0.0), axis=0, keepdims=True)
        dtau += jnp.where(lane == h, jnp.sum(wrk * rq), 0.0)
    dsk = drk * (-0.5 * (rk / sk_row))
    for h in range(H):
        dsk_v[C * h : C * h + C, :] = jnp.broadcast_to(2.0 * to_column(dsk, h), (C, 128))
    dg_bt[...] = dg_b[...].T
    ex_t[0] = dtau
    t_copy = remote(ex_t.at[0], ex_t.at[1], t_s, t_r, 4)
    t_copy.start()

    def phase5(t, carry):
        q = qkvt[t, 0:D, :]
        k = qkvt[t, D : 2 * D, :]
        dq_lo, dq_hi = block_mm(dg_b[...], k)
        dk_lo, dk_hi = block_mm(dg_bt[...], q)
        qf = q.astype(F32)
        kf = k.astype(F32)
        ds = dsq_v[:, 0:1]
        dk = dsk_v[:, 0:1]
        qkvt[t, 0:SPLIT, :] = (dq_lo + ds[0:SPLIT] * qf[0:SPLIT]).astype(BF16)
        qkvt[t, SPLIT:D, :] = (dq_hi + ds[SPLIT:D] * qf[SPLIT:D]).astype(BF16)
        qkvt[t, D : D + SPLIT, :] = (dk_lo + dk[0:SPLIT] * kf[0:SPLIT]).astype(BF16)
        qkvt[t, D + SPLIT : 2 * D, :] = (dk_hi + dk[SPLIT:D] * kf[SPLIT:D]).astype(BF16)
        dw = mm_nt(ut[t], qkvt[t, 0 : 2 * D, :])
        pw[2] += dw[:, 0:D]
        pw[3] += dw[:, D : 2 * D]

        @pl.when(t == 1)
        def _():
            start_b(1)

        @pl.when(t == 6)
        def _():
            start_c(0)

        return carry

    lax.fori_loop(0, nb, phase5, 0)
    start_a(2)
    start_a(3)

    def phase6(t, carry):
        x = x_v[t].astype(F32)
        dy = dy_v[t].astype(F32)
        y_v[t] = (x + mm(ot[t].T, wo_ref[...])).astype(BF16)
        y_out(t).start()
        du_t = mm(wqkv_ref[...], qkvt[t]).astype(BF16)
        du = du_t.T.astype(F32)
        rstd = rstd_v[t][:, 0:1]
        xhat = (x - mean_v[t][:, 0:1]) * rstd
        g = du * gamma
        m1 = jnp.mean(g, axis=-1, keepdims=True)
        m2 = jnp.mean(g * xhat, axis=-1, keepdims=True)
        dx = rstd * (g - m1 - xhat * m2)
        dy_v[t] = (dy + dx).astype(BF16)
        dx_out(t).start()
        dgam = jnp.sum((du * xhat).reshape(TB // 8, 8, D), axis=0)
        dbet = jnp.sum(du.reshape(TB // 8, 8, D), axis=0)
        gb_acc[0] += dgam
        gb_acc[1] += dbet

        @pl.when(t == 1)
        def _():
            start_b(2)
            start_c(1)

        @pl.when(t == 3)
        def _():
            start_b(3)

        @pl.when(t == 5)
        def _():
            start_c(2)

        @pl.when(t == 7)
        def _():
            start_c(3)

        return carry

    lax.fori_loop(0, nb, phase6, 0)

    dgam = jnp.sum(gb_acc[0], axis=0, keepdims=True)
    dbet = jnp.sum(gb_acc[1], axis=0, keepdims=True)
    ex_gb[0] = jnp.concatenate([dgam, dbet, jnp.zeros((6, D), F32)], axis=0)
    for k in range(1, 8):
        small(ex_gb, gb_s, gb_r, k).start()

    for c in range(4):
        stage_c(c).wait_recv()
        total = sb[c] + rc[c]
        if c == 0:
            gwo_ref[...] = total
        else:
            col = {1: 2 * D, 2: 0, 3: D}[c]
            gwqkv_ref[:, col : col + D] = total
    t_copy.wait_recv()
    gtau_ref[...] = (ex_t[0] + ex_t[1])[0:1, 0:H]
    for k in range(1, 8):
        small(ex_gb, gb_s, gb_r, k).wait_recv()
    gb = ((ex_gb[0] + ex_gb[1]) + (ex_gb[2] + ex_gb[3])) + ((ex_gb[4] + ex_gb[5]) + (ex_gb[6] + ex_gb[7]))
    ggam_ref[...] = gb[0:1, :]
    gbet_ref[...] = gb[1:2, :]

    for t in range(nb):
        y_out(t).wait()
        dx_out(t).wait()
    for k in range(1, 4):
        small(ex_g, exg_s, exg_r, k).wait_send()
        small(ex_a, exa_s, exa_r, k).wait_send()
    for c in range(4):
        for xx in range(2):
            stage_a(c, xx).wait_send()
        stage_b(c).wait_send()
        stage_c(c).wait_send()
    t_copy.wait_send()
    for k in range(1, 8):
        small(ex_gb, gb_s, gb_r, k).wait_send()


def solution(mesh):
    act_spec = P(("data", "img"), "seq", None)
    row_spec = P(("data", "seq"), None)
    in_specs = (act_spec, act_spec, P(), P(), P(), P(), P())
    out_specs = (act_spec, act_spec, row_spec, row_spec, P("data"), P("data"), P("data"))

    def local_block(x_in, grad_y, ln_gamma, ln_beta, w_qkv, w_out, head_temp):
        n_tok = x_in.shape[1]
        nb = n_tok // TB
        hbm = pl.BlockSpec(memory_space=pl.ANY)
        vmem = pl.BlockSpec(memory_space=pltpu.VMEM)
        smem = pl.BlockSpec(memory_space=pltpu.SMEM)
        dma = pltpu.SemaphoreType.DMA
        outs = pl.pallas_call(
            functools.partial(kernel, nb),
            out_shape=(
                jax.ShapeDtypeStruct((nb, TB, D), BF16),
                jax.ShapeDtypeStruct((nb, TB, D), BF16),
                jax.ShapeDtypeStruct((ROWS, 3 * D), F32),
                jax.ShapeDtypeStruct((ROWS, D), F32),
                jax.ShapeDtypeStruct((1, D), F32),
                jax.ShapeDtypeStruct((1, D), F32),
                jax.ShapeDtypeStruct((1, H), F32),
            ),
            in_specs=[hbm, hbm, vmem, vmem, vmem, vmem, smem],
            out_specs=(hbm, hbm, vmem, vmem, vmem, vmem, vmem),
            scratch_shapes=[
                pltpu.VMEM((nb, TB, D), BF16),
                pltpu.VMEM((nb, TB, D), BF16),
                pltpu.VMEM((nb, TB, D), BF16),
                pltpu.VMEM((nb, D, TB), BF16),
                pltpu.VMEM((nb, 3 * D, TB), BF16),
                pltpu.VMEM((nb, D, TB), BF16),
                pltpu.VMEM((nb, D, TB), BF16),
                pltpu.VMEM((nb, TB, 128), F32),
                pltpu.VMEM((nb, TB, 128), F32),
                pltpu.VMEM((3 * D, D), BF16),
                pltpu.VMEM((SPLIT, 256), F32),
                pltpu.VMEM((D - SPLIT, 256), F32),
                pltpu.VMEM((D, 128), F32),
                pltpu.VMEM((D, 128), F32),
                pltpu.VMEM((4, C + 8, D), F32),
                pltpu.VMEM((4, C, D), F32),
                pltpu.VMEM((H, C, D), F32),
                pltpu.VMEM((D, D), BF16),
                pltpu.VMEM((D, D), BF16),
                pltpu.VMEM((D, D), BF16),
                pltpu.VMEM((D, D), BF16),
                pltpu.VMEM((D, 128), F32),
                pltpu.VMEM((D, 128), F32),
                pltpu.VMEM((4, D, D), F32),
                pltpu.VMEM((4, 2, ROWS, D), F32),
                pltpu.VMEM((4, 2, ROWS, D), F32),
                pltpu.VMEM((4, ROWS, D), F32),
                pltpu.VMEM((4, ROWS, D), F32),
                pltpu.VMEM((4, ROWS, D), F32),
                pltpu.VMEM((2, 8, D), F32),
                pltpu.VMEM((8, 8, D), F32),
                pltpu.VMEM((2, 8, 128), F32),
                dma((nb,)), dma((nb,)), dma((nb,)), dma((nb,)),
                dma((4,)), dma((4,)), dma((4,)), dma((4,)),
                dma((4, 2)), dma((4, 2)), dma((4,)), dma((4,)), dma((4,)), dma((4,)),
                dma((8,)), dma((8,)), dma, dma,
            ],
            compiler_params=pltpu.CompilerParams(
                collective_id=0, has_side_effects=True, vmem_limit_bytes=64000000
            ),
            name="xca_block",
        )(
            x_in.reshape(nb, TB, D),
            grad_y.reshape(nb, TB, D),
            ln_gamma.reshape(1, D),
            ln_beta.reshape(1, D),
            w_qkv,
            w_out,
            head_temp,
        )
        y, dx, gwqkv, gwo, ggam, gbet, gtau = outs
        return (
            y.reshape(1, n_tok, D),
            dx.reshape(1, n_tok, D),
            gwqkv,
            gwo,
            ggam.reshape(D),
            gbet.reshape(D),
            gtau.reshape(H),
        )

    return jax.shard_map(local_block, mesh=mesh, in_specs=in_specs, out_specs=out_specs, check_vma=False)
```

time: 184 us -> 68.3 us (0.37)
  matrix products: 61.6 us -> 0 us
  Pallas kernels: 0 us -> 54.9 us
  blocking collectives: 37.2 us -> 0 us
  other arithmetic: 34.7 us -> 2.48 us
  waiting for transfers between devices: 24 us -> 0 us
  between operations: 14 us -> 0.65 us
    dot_general x11 -> x0, matrix products: 56.2 us -> none  [the longest x1 10.4 us: local_block(): jnp.einsum('nd,cnhi->dchi', u_act, grad_qkv, preferred_element_type=jnp.f...]
    pallas_call x0 -> x1, Pallas kernels: none -> 54.9 us  [local_block(): pl.pallas_call(functools.partial(kernel, nb), out_shape=(jax.ShapeDtypeSt...]
    psum x3 -> x0, blocking collectives: 37.2 us -> none  [the longest x1 22.6 us: local_block(): grad_gamma, grad_beta = lax.psum((gam_loc, bet_loc), ('img', 'seq'))]
    reduce_sum x7 -> x0, other arithmetic: 15.5 us -> none  [the longest x1 3.54 us: local_block(): sqq_part = jnp.sum(jnp.square(q_act.astype(jnp.float32)), axis=0)]
    psum x2 -> x0, waiting for transfers between devices: 15.2 us -> none  [the longest x1 15.2 us: local_block(): gram_mat, sum_qq, sum_kk = lax.psum((gram_part, sqq_part, skk_part), 'seq')]
    reduce_scatter x2 -> x0, waiting for transfers between devices: 8.7 us -> none  [the longest x1 8.68 us: local_block(): lax.psum_scatter(wqkv_loc, 'seq', scatter_dimension=0, tiled=True)]
    another operation x1 -> x0, other arithmetic: 8.39 us -> none  [local_block(): grad_qkv = jnp.stack([grad_q, grad_k, grad_v]).astype(jnp.bfloat16)]
    broadcast_in_dim x1 -> x0, other arithmetic: 7.34 us -> none  [local_block(): grad_x[None]]
  transfers between devices with their start and end apart: 4 -> 0, of which waited for: 2 -> 0; matrix products, arithmetic and copies ran while one was open for 28% -> 0% of each run, Pallas kernels for 0% -> 0%
where the time goes in v1:
time: 68.3 us; the launch traced here: 68.1 us
  Pallas kernels  54.9 us (80%)
  local copies, waits for them, and re-layouts  10.1 us (15%)
  other arithmetic  2.48 us (4%)
    pallas_call x1, Pallas kernels, local_block(): pl.pallas_call(functools.partial(kernel, nb), out_shape=(jax.ShapeDtypeSt...  54.9 us
    unnamed x13, local copies, waits for them, and re-layouts  7.63 us
    pallas_call x2, other arithmetic, local_block(): pl.pallas_call(functools.partial(kernel, nb), out_shape=(jax.ShapeDtypeSt...  2.48 us

profile of v1, /device:TPU:0, one launch (start us, length us, event | category | flops | bytes accessed | tf_op | source)
XLA Modules:
  0.0 68.1 jit_solution(15734445121179419702)
XLA Ops:
  0.6 1.2 %reshape.43.gamma_ref = f32[1,384]{1,0:T(1,128)} reshape(f32[384]{0:T(512)} %param.9) | data formatting | bytes 3072 | tf_op jit(solution)/shard_map/reshape | solution.py:463
  1.9 1.2 %reshape.44.beta_ref = f32[1,384]{1,0:T(1,128)} reshape(f32[384]{0:T(512)} %param.10) | data formatting | bytes 3072 | tf_op jit(solution)/shard_map/reshape | solution.py:464
  3.1 54.9 %xca_block.1 = (bf16[8,512,384]{2,1,0:T(8,128)(2,1)}, bf16[8,512,384]{2,1,0:T(8,128)(2,1)}, f32[96,1152]{1,0:T(8,128)}, f32[96,384]{1,0:T(8,128)}, f32[1,384]{1,...) custom-call(bf16[8,512,384]{2,1,0:T(8,128)(2,1)} %bitcast.5, bf16[8,512,384]{2,1,0:T(8,128)(2,1)} %bitcast.6, ...), custom_call_target="tpu_custom_call" | custom-call | tf_op jit(solution)/shard_map/xca_block/pallas_call | solution.py:405
  58.0 1.3 %reduce = f32[384]{0:T(512)} reduce(f32[1,384]{1,0:T(1,128)} %get-tuple-element.18, f32[]{:T(128)} %constant.2), dimensions={0}, to_apply=%get-tuple-element.18.reduce_sub_computation | reduce | bytes 3076 | tf_op jit(solution)/shard_map/xca_block/pallas_call | solution.py:405
  59.3 1.2 %reduce.1 = f32[384]{0:T(512)} reduce(f32[1,384]{1,0:T(1,128)} %get-tuple-element.19, f32[]{:T(128)} %constant.2), dimensions={0}, to_apply=%get-tuple-element.19.reduce_sub_computation | reduce | bytes 3076 | tf_op jit(solution)/shard_map/xca_block/pallas_call | solution.py:405
  60.5 0.0 copy-start
  60.5 4.0 %copy.19 = bf16[1,4096,384]{2,1,0:T(8,128)(2,1)} copy(bf16[1,4096,384]{2,1,0:T(8,128)(2,1)} %bitcast.8) | data formatting | bytes 6291456
  64.5 0.0 copy-done
  64.5 0.0 copy-start.1
  64.5 0.0 copy-start.2
  64.5 0.0 copy-start.3
  64.5 1.7 %copy.20 = bf16[1,4096,384]{2,1,0:T(8,128)(2,1)} copy(bf16[1,4096,384]{2,1,0:T(8,128)(2,1)S(1)} %bitcast.7) | data formatting | bytes 6291456
  66.2 0.0 copy-done.1
  66.2 0.8 %copy.21 = f32[96,1152]{1,0:T(8,128)} copy(f32[96,1152]{1,0:T(8,128)S(1)} %copy-done.1) | data formatting | bytes 884736
  67.0 0.0 copy-done.2
  67.0 0.7 copy.22
  67.6 0.0 copy-done.3
  67.6 0.5 copy.23
Async XLA Ops:
  60.5 4.0 %copy-start = (bf16[8,512,384]{2,1,0:T(8,128)(2,1)S(1)}, bf16[8,512,384]{2,1,0:T(8,128)(2,1)}, u32[]{:S(2)}) copy-start(bf16[8,512,384]{2,1,0:T(8,128)(2,1)} %get-tuple-element.15) | copy-start | bytes 9437188
  64.5 1.7 %copy-start.1 = (f32[96,1152]{1,0:T(8,128)S(1)}, f32[96,1152]{1,0:T(8,128)}, u32[]{:S(2)}) copy-start(f32[96,1152]{1,0:T(8,128)} %get-tuple-element.30) | copy-start | bytes 1327108
  64.5 2.4 %copy-start.2 = (f32[96,384]{1,0:T(8,128)S(1)}, f32[96,384]{1,0:T(8,128)}, u32[]{:S(2)}) copy-start(f32[96,384]{1,0:T(8,128)} %get-tuple-element.31) | copy-start | bytes 442372
  64.5 3.1 %copy-start.3 = (f32[1,8]{1,0:T(1,128)S(1)}, f32[1,8]{1,0:T(1,128)}, u32[]{:S(2)}) copy-start(f32[1,8]{1,0:T(1,128)} %get-tuple-element.20) | copy-start | bytes 100

commit v2 on v1

--- a/solution.py
+++ b/solution.py
@@ -18,7 +18,14 @@
 SPLIT = 240
 OFF = 128
 ROWS = 96
-TB = 512
+TB = 1024
+S4B0 = 1
+S5B1 = 0
+S5C0 = 3
+S6B2 = 0
+S6B3 = 1
+S6C2 = 2
+S6C3 = 3
 
 
 def mm(a, b):
@@ -66,11 +73,11 @@
 def kernel(
     nb,
     x_hbm, dy_hbm, gamma_ref, beta_ref, wqkv_ref, wo_ref, tau_ref,
-    y_hbm, dx_hbm, gwqkv_ref, gwo_ref, ggam_ref, gbet_ref, gtau_ref,
-    x_v, dy_v, y_v, ut, qkvt, dot_v, ot, mean_v, rstd_v, wqkvt,
+    y_v, dx_v, gwqkv_ref, gwo_ref, ggam_ref, gbet_ref, gtau_ref,
+    x_v, dy_v, ut, qkvt, dot_v, ot, mean_v, rstd_v, wqkvt,
     g_lo, g_hi, sq_acc, sk_acc, ex_g, ex_a, a_f, a_b, a_bt, dg_b, dg_bt, dsq_v, dsk_v,
     pw, ra, sa, rb, sb, rc, gb_acc, ex_gb, ex_t,
-    x_sem, dy_sem, y_sem, dx_sem,
+    x_sem, dy_sem,
     exg_s, exg_r, exa_s, exa_r, a_s, a_r, b_s, b_r, c_s, c_r, gb_s, gb_r, t_s, t_r,
 ):
     data = lax.axis_index("data")
@@ -95,12 +102,6 @@
     def dy_in(t):
         return pltpu.make_async_copy(dy_hbm.at[t], dy_v.at[t], dy_sem.at[t])
 
-    def y_out(t):
-        return pltpu.make_async_copy(y_v.at[t], y_hbm.at[t], y_sem.at[t])
-
-    def dx_out(t):
-        return pltpu.make_async_copy(dy_v.at[t], dx_hbm.at[t], dx_sem.at[t])
-
     for t in range(nb):
         x_in(t).start()
     for t in range(nb):
@@ -143,8 +144,8 @@
     wqkvt[...] = wqkv_ref[...].T
     for ref in (g_lo, g_hi, sq_acc, sk_acc, gb_acc, pw):
         ref[...] = jnp.zeros_like(ref)
-    gamma = gamma_ref[...]
-    beta = beta_ref[...]
+    gamma = gamma_ref[...].reshape(1, D)
+    beta = beta_ref[...].reshape(1, D)
 
     def lane_fold(a):
         out = a[:, 0:128]
@@ -241,7 +242,7 @@
         qkvt[t, 2 * D + SPLIT : 3 * D, :] = dv_hi.astype(BF16)
         pw[1] += mm_nt(ut[t], qkvt[t, 2 * D : 3 * D, :])
 
-        @pl.when(t == 3)
+        @pl.when(t == S4B0)
         def _():
             start_b(0)
 
@@ -296,11 +297,11 @@
         pw[2] += dw[:, 0:D]
         pw[3] += dw[:, D : 2 * D]
 
-        @pl.when(t == 1)
+        @pl.when(t == S5B1)
         def _():
             start_b(1)
 
-        @pl.when(t == 6)
+        @pl.when(t == S5C0)
         def _():
             start_c(0)
 
@@ -314,7 +315,6 @@
         x = x_v[t].astype(F32)
         dy = dy_v[t].astype(F32)
         y_v[t] = (x + mm(ot[t].T, wo_ref[...])).astype(BF16)
-        y_out(t).start()
         du_t = mm(wqkv_ref[...], qkvt[t]).astype(BF16)
         du = du_t.T.astype(F32)
         rstd = rstd_v[t][:, 0:1]
@@ -323,27 +323,26 @@
         m1 = jnp.mean(g, axis=-1, keepdims=True)
         m2 = jnp.mean(g * xhat, axis=-1, keepdims=True)
         dx = rstd * (g - m1 - xhat * m2)
-        dy_v[t] = (dy + dx).astype(BF16)
-        dx_out(t).start()
+        dx_v[t] = (dy + dx).astype(BF16)
         dgam = jnp.sum((du * xhat).reshape(TB // 8, 8, D), axis=0)
         dbet = jnp.sum(du.reshape(TB // 8, 8, D), axis=0)
         gb_acc[0] += dgam
         gb_acc[1] += dbet
 
-        @pl.when(t == 1)
+        @pl.when(t == S6B2)
         def _():
             start_b(2)
             start_c(1)
 
-        @pl.when(t == 3)
+        @pl.when(t == S6B3)
         def _():
             start_b(3)
 
-        @pl.when(t == 5)
+        @pl.when(t == S6C2)
         def _():
             start_c(2)
 
-        @pl.when(t == 7)
+        @pl.when(t == S6C3)
         def _():
             start_c(3)
 
@@ -366,16 +365,13 @@
             col = {1: 2 * D, 2: 0, 3: D}[c]
             gwqkv_ref[:, col : col + D] = total
     t_copy.wait_recv()
-    gtau_ref[...] = (ex_t[0] + ex_t[1])[0:1, 0:H]
+    gtau_ref[...] = (ex_t[0] + ex_t[1])[0, 0:H]
     for k in range(1, 8):
         small(ex_gb, gb_s, gb_r, k).wait_recv()
     gb = ((ex_gb[0] + ex_gb[1]) + (ex_gb[2] + ex_gb[3])) + ((ex_gb[4] + ex_gb[5]) + (ex_gb[6] + ex_gb[7]))
-    ggam_ref[...] = gb[0:1, :]
-    gbet_ref[...] = gb[1:2, :]
-
-    for t in range(nb):
-        y_out(t).wait()
-        dx_out(t).wait()
+    ggam_ref[...] = gb[0]
+    gbet_ref[...] = gb[1]
+
     for k in range(1, 4):
         small(ex_g, exg_s, exg_r, k).wait_send()
         small(ex_a, exa_s, exa_r, k).wait_send()
@@ -389,6 +385,15 @@
         small(ex_gb, gb_s, gb_r, k).wait_send()
 
 
+def store_kernel(*refs):
+    sem = refs[14]
+    copies = [pltpu.make_async_copy(refs[i], refs[7 + i], sem.at[i]) for i in range(7)]
+    for copy in copies:
+        copy.start()
+    for copy in copies:
+        copy.wait()
+
+
 def solution(mesh):
     act_spec = P(("data", "img"), "seq", None)
     row_spec = P(("data", "seq"), None)
@@ -405,18 +410,17 @@
         outs = pl.pallas_call(
             functools.partial(kernel, nb),
             out_shape=(
-                jax.ShapeDtypeStruct((nb, TB, D), BF16),
-                jax.ShapeDtypeStruct((nb, TB, D), BF16),
-                jax.ShapeDtypeStruct((ROWS, 3 * D), F32),
-                jax.ShapeDtypeStruct((ROWS, D), F32),
-                jax.ShapeDtypeStruct((1, D), F32),
-                jax.ShapeDtypeStruct((1, D), F32),
-                jax.ShapeDtypeStruct((1, H), F32),
+                pltpu.VMEM((nb, TB, D), BF16),
+                pltpu.VMEM((nb, TB, D), BF16),
+                pltpu.VMEM((ROWS, 3 * D), F32),
+                pltpu.VMEM((ROWS, D), F32),
+                pltpu.VMEM((D,), F32),
+                pltpu.VMEM((D,), F32),
+                pltpu.VMEM((H,), F32),
             ),
             in_specs=[hbm, hbm, vmem, vmem, vmem, vmem, smem],
-            out_specs=(hbm, hbm, vmem, vmem, vmem, vmem, vmem),
+            out_specs=(vmem,) * 7,
             scratch_shapes=[
-                pltpu.VMEM((nb, TB, D), BF16),
                 pltpu.VMEM((nb, TB, D), BF16),
                 pltpu.VMEM((nb, TB, D), BF16),
                 pltpu.VMEM((nb, D, TB), BF16),
@@ -448,33 +452,42 @@
                 pltpu.VMEM((2, 8, D), F32),
                 pltpu.VMEM((8, 8, D), F32),
                 pltpu.VMEM((2, 8, 128), F32),
-                dma((nb,)), dma((nb,)), dma((nb,)), dma((nb,)),
+                dma((nb,)), dma((nb,)),
                 dma((4,)), dma((4,)), dma((4,)), dma((4,)),
                 dma((4, 2)), dma((4, 2)), dma((4,)), dma((4,)), dma((4,)), dma((4,)),
                 dma((8,)), dma((8,)), dma, dma,
             ],
             compiler_params=pltpu.CompilerParams(
-                collective_id=0, has_side_effects=True, vmem_limit_bytes=64000000
+                collective_id=0, has_side_effects=True, vmem_limit_bytes=52000000
             ),
             name="xca_block",
         )(
             x_in.reshape(nb, TB, D),
             grad_y.reshape(nb, TB, D),
-            ln_gamma.reshape(1, D),
-            ln_beta.reshape(1, D),
+            ln_gamma,
+            ln_beta,
             w_qkv,
             w_out,
             head_temp,
         )
+        outs = pl.pallas_call(
+            store_kernel,
+            out_shape=(
+                jax.ShapeDtypeStruct((nb, TB, D), BF16),
+                jax.ShapeDtypeStruct((nb, TB, D), BF16),
+                jax.ShapeDtypeStruct((ROWS, 3 * D), F32),
+                jax.ShapeDtypeStruct((ROWS, D), F32),
+                jax.ShapeDtypeStruct((D,), F32),
+                jax.ShapeDtypeStruct((D,), F32),
+                jax.ShapeDtypeStruct((H,), F32),
+            ),
+            in_specs=[hbm] * 7,
+            out_specs=(hbm,) * 7,
+            scratch_shapes=[dma((7,))],
+            compiler_params=pltpu.CompilerParams(vmem_limit_bytes=4 * 2**20),
+            name="xca_store",
+        )(*outs)
         y, dx, gwqkv, gwo, ggam, gbet, gtau = outs
-        return (
-            y.reshape(1, n_tok, D),
-            dx.reshape(1, n_tok, D),
-            gwqkv,
-            gwo,
-            ggam.reshape(D),
-            gbet.reshape(D),
-            gtau.reshape(H),
-        )
+        return y.reshape(1, n_tok, D), dx.reshape(1, n_tok, D), gwqkv, gwo, ggam, gbet, gtau
 
     return jax.shard_map(local_block, mesh=mesh, in_specs=in_specs, out_specs=out_specs, check_vma=False)

time: 68.3 us -> 50.6 us (0.74)
  local copies, waits for them, and re-layouts: 10.1 us -> 0 us
  Pallas kernels: 54.9 us -> 49.9 us
  other arithmetic: 2.48 us -> 0 us
    unnamed x13 -> x0, local copies, waits for them, and re-layouts: 7.63 us -> none
    pallas_call x1 -> x2, Pallas kernels: 54.9 us -> 49.9 us  [the longest x1 47 us: local_block(): pl.pallas_call(functools.partial(kernel, nb), out_shape=(pltpu.VMEM((nb,...]
    reshape x2 -> x0, local copies, waits for them, and re-layouts: 2.49 us -> none  [the longest x1 1.25 us: local_block(): ln_gamma.reshape(1, D)]
    pallas_call x2 -> x0, other arithmetic: 2.48 us -> none  [local_block(): pl.pallas_call(functools.partial(kernel, nb), out_shape=(jax.ShapeDtypeSt...]
where the time goes in v2:
time: 50.6 us; the launch traced here: 50.5 us
  Pallas kernels  49.9 us (99%)
  between operations  0.64 us (1%)
    pallas_call x1, Pallas kernels, local_block(): pl.pallas_call(functools.partial(kernel, nb), out_shape=(pltpu.VMEM((nb,...  47 us
    pallas_call x1, Pallas kernels, local_block(): pl.pallas_call(store_kernel, out_shape=(jax.ShapeDtypeStruct((nb, TB, D),...  2.94 us

profile of v2, /device:TPU:0, one launch (start us, length us, event | category | flops | bytes accessed | tf_op | source)
XLA Modules:
  0.0 50.5 jit_solution(8866841119157640479)
XLA Ops:
  0.6 47.0 %xca_block.1 = (bf16[4,1024,384]{2,1,0:T(8,128)(2,1)S(1)}, bf16[4,1024,384]{2,1,0:T(8,128)(2,1)S(1)}, f32[96,1152]{1,0:T(8,128)S(1)}, f32[96,384]{1,0:T(8,128)S(...) custom-call(bf16[4,1024,384]{2,1,0:T(8,128)(2,1)} %bitcast.4, bf16[4,1024,384]{2,1,0:T(8,128)(2,1)} %bitcast.5, ...), custom_call_target="tpu_custom_call" | custom-call | tf_op jit(solution)/shard_map/xca_block/pallas_call | solution.py:410
  47.6 2.9 %xca_store.1 = (bf16[4,1024,384]{2,1,0:T(8,128)(2,1)}, bf16[4,1024,384]{2,1,0:T(8,128)(2,1)}, f32[96,1152]{1,0:T(8,128)}, f32[96,384]{1,0:T(8,128)}, f32[384]{0:T(512)}, /*index=5*/f32[384]{0:T(512)}, f32[8]{0:T(128)}) custom-call(bf16[4,1024,384]{2,1,0:T(8,128)(2,1)S(1)} %get-tuple-element.21.refs_0_, bf16[4,1024,384]{2,1,0:T(8,128)(2,1)S(1)} %get-tuple-element.22.refs_1_, ...), custom_call_target="tpu_custom_call" | custom-call | tf_op jit(solution)/shard_map/xca_store/pallas_call | solution.py:473

commit v3 on v2

--- a/solution.py
+++ b/solution.py
@@ -19,13 +19,7 @@
 OFF = 128
 ROWS = 96
 TB = 1024
-S4B0 = 1
-S5B1 = 0
-S5C0 = 3
-S6B2 = 0
-S6B3 = 1
-S6C2 = 2
-S6C3 = 3
+HALVES = (1, 1, 1, 2)
 
 
 def mm(a, b):
@@ -72,12 +66,13 @@
 
 def kernel(
     nb,
-    x_hbm, dy_hbm, gamma_ref, beta_ref, wqkv_ref, wo_ref, tau_ref,
+    x_hbm, dy_hbm, gamma_hbm, beta_hbm, wqkv_hbm, wo_hbm, tau_hbm,
     y_v, dx_v, gwqkv_ref, gwo_ref, ggam_ref, gbet_ref, gtau_ref,
     x_v, dy_v, ut, qkvt, dot_v, ot, mean_v, rstd_v, wqkvt,
-    g_lo, g_hi, sq_acc, sk_acc, ex_g, ex_a, a_f, a_b, a_bt, dg_b, dg_bt, dsq_v, dsk_v,
+    gamma_ref, beta_ref, wqkv_ref, wo_ref, tau_ref,
+    g_lo, g_hi, sq_acc, sk_acc, ex_g, ex_h, ex_a, a_f, a_b, a_bt, dg_b, dg_bt, dsq_v, dsk_v,
     pw, ra, sa, rb, sb, rc, gb_acc, ex_gb, ex_t,
-    x_sem, dy_sem,
+    x_sem, dy_sem, in_sem,
     exg_s, exg_r, exa_s, exa_r, a_s, a_r, b_s, b_r, c_s, c_r, gb_s, gb_r, t_s, t_r,
 ):
     data = lax.axis_index("data")
@@ -102,8 +97,15 @@
     def dy_in(t):
         return pltpu.make_async_copy(dy_hbm.at[t], dy_v.at[t], dy_sem.at[t])
 
+    def weight_in(i):
+        pairs = ((wqkv_hbm, wqkv_ref), (gamma_hbm, gamma_ref), (beta_hbm, beta_ref), (wo_hbm, wo_ref), (tau_hbm, tau_ref))
+        return pltpu.make_async_copy(*pairs[i], in_sem.at[i])
+
+    weight_in(0).start()
     for t in range(nb):
         x_in(t).start()
+    for i in range(1, 5):
+        weight_in(i).start()
     for t in range(nb):
         dy_in(t).start()
 
@@ -119,11 +121,14 @@
         rows = pl.ds(pl.multiple_of(ROWS * (2 * xx + 1 - core), 8), ROWS)
         return remote(pw.at[c, rows, :], ra.at[c, xx], a_s.at[c, xx], a_r.at[c, xx], 1)
 
-    def stage_b(c):
-        return remote(sa.at[c, 1 - xc], rb.at[c], b_s.at[c], b_r.at[c], 2)
-
-    def stage_c(c):
-        return remote(sb.at[c], rc.at[c], c_s.at[c], c_r.at[c], 4)
+    def part(c, h):
+        return pl.ds(h * (ROWS // HALVES[c]), ROWS // HALVES[c])
+
+    def stage_b(c, h):
+        return remote(sa.at[c, 1 - xc, part(c, h)], rb.at[c, part(c, h)], b_s.at[c, h], b_r.at[c, h], 2)
+
+    def stage_c(c, h):
+        return remote(sb.at[c, part(c, h)], rc.at[c, part(c, h)], c_s.at[c, h], c_r.at[c, h], 4)
 
     def start_a(c):
         for xx in range(2):
@@ -134,16 +139,25 @@
             stage_a(c, xx).wait_recv()
             rows = pl.ds(pl.multiple_of(ROWS * (2 * xx + core), 8), ROWS)
             sa[c, xx] = pw[c, rows, :] + ra[c, xx]
-        stage_b(c).start()
-
-    def start_c(c):
-        stage_b(c).wait_recv()
-        sb[c] = sa[c, xc] + rb[c]
-        stage_c(c).start()
-
-    wqkvt[...] = wqkv_ref[...].T
+        for h in range(HALVES[c]):
+            stage_b(c, h).start()
+
+    def start_c(c, h=0):
+        stage_b(c, h).wait_recv()
+        sb[c, part(c, h)] = sa[c, xc, part(c, h)] + rb[c, part(c, h)]
+        stage_c(c, h).start()
+
+    def loop(body, steps):
+        for t in range(nb):
+            body(t)
+            if (t + 1) * 4 % nb == 0 and (t + 1) * 4 // nb - 1 in steps:
+                steps[(t + 1) * 4 // nb - 1]()
+
     for ref in (g_lo, g_hi, sq_acc, sk_acc, gb_acc, pw):
         ref[...] = jnp.zeros_like(ref)
+    for i in range(3):
+        weight_in(i).wait()
+    wqkvt[...] = wqkv_ref[...].T
     gamma = gamma_ref[...].reshape(1, D)
     beta = beta_ref[...].reshape(1, D)
 
@@ -153,7 +167,7 @@
             out = out + a[:, 128 * i : 128 * i + 128]
         return out
 
-    def phase1(t, carry):
+    def phase1(t):
         x_in(t).wait()
         x = x_v[t].astype(F32)
         mean = jnp.mean(x, axis=-1, keepdims=True)
@@ -175,9 +189,8 @@
         kf = k.astype(F32)
         sq_acc[...] += lane_fold(qf * qf)
         sk_acc[...] += lane_fold(kf * kf)
-        return carry
-
-    lax.fori_loop(0, nb, phase1, 0)
+
+    loop(phase1, {})
 
     ex_g[0, 0:C, :] = pack(g_lo[...], g_hi[...])
     sq_row = jnp.zeros((1, D), F32)
@@ -188,13 +201,21 @@
         sk_row += to_row(jnp.sum(sk_acc[rows, :], axis=1, keepdims=True), h)
     ex_g[0, C : C + 8, :] = jnp.concatenate([sq_row, sk_row, jnp.zeros((6, D), F32)], axis=0)
     pl.semaphore_wait(barrier, 7)
-    for k in range(1, 4):
-        small(ex_g, exg_s, exg_r, k).start()
+    g_core = remote(ex_g.at[0], ex_g.at[1], exg_s.at[0], exg_r.at[0], 1)
+    g_chip = remote(ex_h.at[0], ex_h.at[1], exg_s.at[1], exg_r.at[1], 2)
+    g_core.start()
+    for i in range(3, 5):
+        weight_in(i).wait()
+
+    def gram_step():
+        g_core.wait_recv()
+        ex_h[0] = ex_g[0] + ex_g[1]
+        g_chip.start()
 
     g_lo[...] = jnp.zeros_like(g_lo)
     g_hi[...] = jnp.zeros_like(g_hi)
 
-    def phase2(t, carry):
+    def phase2(t):
         dy_in(t).wait()
         v = mm(wqkvt[2 * D : 3 * D, :], ut[t]).astype(BF16)
         qkvt[t, 2 * D : 3 * D, :] = v
@@ -202,16 +223,14 @@
         dot_v[t] = do
         g_lo[...] += mm_nt(do[0:SPLIT, :], v[0:256, :])
         g_hi[...] += mm_nt(do[SPLIT:D, :], v[OFF:D, :])
-        return carry
-
-    lax.fori_loop(0, nb, phase2, 0)
+
+    loop(phase2, {0: gram_step})
     ex_a[0] = pack(g_lo[...], g_hi[...])
     for k in range(1, 4):
         small(ex_a, exa_s, exa_r, k).start()
 
-    for k in range(1, 4):
-        small(ex_g, exg_s, exg_r, k).wait_recv()
-    gram_all = (ex_g[0] + ex_g[1]) + (ex_g[2] + ex_g[3])
+    g_chip.wait_recv()
+    gram_all = ex_h[0] + ex_h[1]
     gram = gram_all[0:C, :]
     sq_row = gram_all[C : C + 1, :]
     sk_row = gram_all[C + 1 : C + 2, :]
@@ -226,29 +245,22 @@
         a_b[C * h : C * h + C, :] = a.astype(BF16)
     a_bt[...] = a_b[...].T
 
-    def phase3(t, carry):
+    def phase3(t):
         o_lo, o_hi = block_mm(a_b[...], qkvt[t, 2 * D : 3 * D, :])
         ot[t, 0:SPLIT, :] = o_lo.astype(BF16)
         ot[t, SPLIT:D, :] = o_hi.astype(BF16)
         pw[0] += mm(ot[t], dy_v[t])
-        return carry
-
-    lax.fori_loop(0, nb, phase3, 0)
+
+    loop(phase3, {})
     start_a(0)
 
-    def phase4(t, carry):
+    def phase4(t):
         dv_lo, dv_hi = block_mm(a_bt[...], dot_v[t])
         qkvt[t, 2 * D : 2 * D + SPLIT, :] = dv_lo.astype(BF16)
         qkvt[t, 2 * D + SPLIT : 3 * D, :] = dv_hi.astype(BF16)
         pw[1] += mm_nt(ut[t], qkvt[t, 2 * D : 3 * D, :])
 
-        @pl.when(t == S4B0)
-        def _():
-            start_b(0)
-
-        return carry
-
-    lax.fori_loop(0, nb, phase4, 0)
+    loop(phase4, {1: lambda: start_b(0)})
     start_a(1)
 
     for k in range(1, 4):
@@ -280,75 +292,49 @@
     t_copy = remote(ex_t.at[0], ex_t.at[1], t_s, t_r, 4)
     t_copy.start()
 
-    def phase5(t, carry):
-        q = qkvt[t, 0:D, :]
-        k = qkvt[t, D : 2 * D, :]
-        dq_lo, dq_hi = block_mm(dg_b[...], k)
-        dk_lo, dk_hi = block_mm(dg_bt[...], q)
-        qf = q.astype(F32)
-        kf = k.astype(F32)
+    def phase5(t):
+        dq_lo, dq_hi = block_mm(dg_b[...], qkvt[t, D : 2 * D, :])
+        qf = qkvt[t, 0:D, :].astype(F32)
         ds = dsq_v[:, 0:1]
-        dk = dsk_v[:, 0:1]
-        qkvt[t, 0:SPLIT, :] = (dq_lo + ds[0:SPLIT] * qf[0:SPLIT]).astype(BF16)
-        qkvt[t, SPLIT:D, :] = (dq_hi + ds[SPLIT:D] * qf[SPLIT:D]).astype(BF16)
-        qkvt[t, D : D + SPLIT, :] = (dk_lo + dk[0:SPLIT] * kf[0:SPLIT]).astype(BF16)
-        qkvt[t, D + SPLIT : 2 * D, :] = (dk_hi + dk[SPLIT:D] * kf[SPLIT:D]).astype(BF16)
-        dw = mm_nt(ut[t], qkvt[t, 0 : 2 * D, :])
-        pw[2] += dw[:, 0:D]
-        pw[3] += dw[:, D : 2 * D]
-
-        @pl.when(t == S5B1)
-        def _():
-            start_b(1)
-
-        @pl.when(t == S5C0)
-        def _():
-            start_c(0)
-
-        return carry
-
-    lax.fori_loop(0, nb, phase5, 0)
+        dot_v[t, 0:SPLIT, :] = (dq_lo + ds[0:SPLIT] * qf[0:SPLIT]).astype(BF16)
+        dot_v[t, SPLIT:D, :] = (dq_hi + ds[SPLIT:D] * qf[SPLIT:D]).astype(BF16)
+        pw[2] += mm_nt(ut[t], dot_v[t])
+
+    loop(phase5, {0: lambda: start_b(1), 3: lambda: start_c(0)})
     start_a(2)
+
+    def phase6(t):
+        dk_lo, dk_hi = block_mm(dg_bt[...], qkvt[t, 0:D, :])
+        kf = qkvt[t, D : 2 * D, :].astype(F32)
+        ds = dsk_v[:, 0:1]
+        qkvt[t, D : D + SPLIT, :] = (dk_lo + ds[0:SPLIT] * kf[0:SPLIT]).astype(BF16)
+        qkvt[t, D + SPLIT : 2 * D, :] = (dk_hi + ds[SPLIT:D] * kf[SPLIT:D]).astype(BF16)
+        pw[3] += mm_nt(ut[t], qkvt[t, D : 2 * D, :])
+
+    loop(phase6, {1: lambda: start_b(2), 2: lambda: start_c(1)})
     start_a(3)
 
-    def phase6(t, carry):
-        x = x_v[t].astype(F32)
-        dy = dy_v[t].astype(F32)
-        y_v[t] = (x + mm(ot[t].T, wo_ref[...])).astype(BF16)
-        du_t = mm(wqkv_ref[...], qkvt[t]).astype(BF16)
-        du = du_t.T.astype(F32)
+    def phase7(t):
+        du_t = mm(wqkv_ref[:, 0:D], dot_v[t]) + mm(wqkv_ref[:, D : 3 * D], qkvt[t, D : 3 * D, :])
+        du = du_t.astype(BF16).T.astype(F32)
         rstd = rstd_v[t][:, 0:1]
-        xhat = (x - mean_v[t][:, 0:1]) * rstd
+        xhat = (x_v[t].astype(F32) - mean_v[t][:, 0:1]) * rstd
         g = du * gamma
         m1 = jnp.mean(g, axis=-1, keepdims=True)
         m2 = jnp.mean(g * xhat, axis=-1, keepdims=True)
         dx = rstd * (g - m1 - xhat * m2)
-        dx_v[t] = (dy + dx).astype(BF16)
-        dgam = jnp.sum((du * xhat).reshape(TB // 8, 8, D), axis=0)
-        dbet = jnp.sum(du.reshape(TB // 8, 8, D), axis=0)
-        gb_acc[0] += dgam
-        gb_acc[1] += dbet
-
-        @pl.when(t == S6B2)
-        def _():
-            start_b(2)
-            start_c(1)
-
-        @pl.when(t == S6B3)
-        def _():
-            start_b(3)
-
-        @pl.when(t == S6C2)
-        def _():
-            start_c(2)
-
-        @pl.when(t == S6C3)
-        def _():
-            start_c(3)
-
-        return carry
-
-    lax.fori_loop(0, nb, phase6, 0)
+        dx_v[t] = (dy_v[t].astype(F32) + dx).astype(BF16)
+        gb_acc[0] += jnp.sum((du * xhat).reshape(TB // 8, 8, D), axis=0)
+        gb_acc[1] += jnp.sum(du.reshape(TB // 8, 8, D), axis=0)
+
+    loop(
+        phase7,
+        {
+            0: lambda: start_b(3),
+            1: lambda: start_c(2),
+            2: lambda: start_c(3, 0),
+            3: lambda: start_c(3, 1),
+        })
 
     dgam = jnp.sum(gb_acc[0], axis=0, keepdims=True)
     dbet = jnp.sum(gb_acc[1], axis=0, keepdims=True)
@@ -356,8 +342,14 @@
     for k in range(1, 8):
         small(ex_gb, gb_s, gb_r, k).start()
 
+    def phase8(t):
+        y_v[t] = (x_v[t].astype(F32) + mm(ot[t].T, wo_ref[...])).astype(BF16)
+
+    loop(phase8, {})
+
     for c in range(4):
-        stage_c(c).wait_recv()
+        for h in range(HALVES[c]):
+            stage_c(c, h).wait_recv()
         total = sb[c] + rc[c]
         if c == 0:
             gwo_ref[...] = total
@@ -373,13 +365,15 @@
     gbet_ref[...] = gb[1]
 
     for k in range(1, 4):
-        small(ex_g, exg_s, exg_r, k).wait_send()
         small(ex_a, exa_s, exa_r, k).wait_send()
     for c in range(4):
         for xx in range(2):
             stage_a(c, xx).wait_send()
-        stage_b(c).wait_send()
-        stage_c(c).wait_send()
+        for h in range(HALVES[c]):
+            stage_b(c, h).wait_send()
+            stage_c(c, h).wait_send()
+    g_core.wait_send()
+    g_chip.wait_send()
     t_copy.wait_send()
     for k in range(1, 8):
         small(ex_gb, gb_s, gb_r, k).wait_send()
@@ -405,7 +399,6 @@
         nb = n_tok // TB
         hbm = pl.BlockSpec(memory_space=pl.ANY)
         vmem = pl.BlockSpec(memory_space=pltpu.VMEM)
-        smem = pl.BlockSpec(memory_space=pltpu.SMEM)
         dma = pltpu.SemaphoreType.DMA
         outs = pl.pallas_call(
             functools.partial(kernel, nb),
@@ -418,7 +411,7 @@
                 pltpu.VMEM((D,), F32),
                 pltpu.VMEM((H,), F32),
             ),
-            in_specs=[hbm, hbm, vmem, vmem, vmem, vmem, smem],
+            in_specs=[hbm] * 7,
             out_specs=(vmem,) * 7,
             scratch_shapes=[
                 pltpu.VMEM((nb, TB, D), BF16),
@@ -430,11 +423,17 @@
                 pltpu.VMEM((nb, TB, 128), F32),
                 pltpu.VMEM((nb, TB, 128), F32),
                 pltpu.VMEM((3 * D, D), BF16),
+                pltpu.VMEM((D,), F32),
+                pltpu.VMEM((D,), F32),
+                pltpu.VMEM((D, 3 * D), BF16),
+                pltpu.VMEM((D, D), BF16),
+                pltpu.SMEM((H,), F32),
                 pltpu.VMEM((SPLIT, 256), F32),
                 pltpu.VMEM((D - SPLIT, 256), F32),
                 pltpu.VMEM((D, 128), F32),
                 pltpu.VMEM((D, 128), F32),
-                pltpu.VMEM((4, C + 8, D), F32),
+                pltpu.VMEM((2, C + 8, D), F32),
+                pltpu.VMEM((2, C + 8, D), F32),
                 pltpu.VMEM((4, C, D), F32),
                 pltpu.VMEM((H, C, D), F32),
                 pltpu.VMEM((D, D), BF16),
@@ -452,9 +451,9 @@
                 pltpu.VMEM((2, 8, D), F32),
                 pltpu.VMEM((8, 8, D), F32),
                 pltpu.VMEM((2, 8, 128), F32),
-                dma((nb,)), dma((nb,)),
-                dma((4,)), dma((4,)), dma((4,)), dma((4,)),
-                dma((4, 2)), dma((4, 2)), dma((4,)), dma((4,)), dma((4,)), dma((4,)),
+                dma((nb,)), dma((nb,)), dma((5,)),
+                dma((2,)), dma((2,)), dma((4,)), dma((4,)),
+                dma((4, 2)), dma((4, 2)), dma((4, 2)), dma((4, 2)), dma((4, 2)), dma((4, 2)),
                 dma((8,)), dma((8,)), dma, dma,
             ],
             compiler_params=pltpu.CompilerParams(

time: 50.6 us -> 47.5 us (0.939)
  Pallas kernels: 49.9 us -> 46.6 us
    pallas_call x1, Pallas kernels: 47 us -> 43.7 us  [local_block(): pl.pallas_call(functools.partial(kernel, nb), out_shape=(pltpu.VMEM((nb,...]
where the time goes in v3:
time: 47.5 us; the launch traced here: 47.4 us
  Pallas kernels  46.6 us (98%)
  between operations  0.82 us (2%)
    pallas_call x1, Pallas kernels, local_block(): pl.pallas_call(functools.partial(kernel, nb), out_shape=(pltpu.VMEM((nb,...  43.7 us
    pallas_call x1, Pallas kernels, local_block(): pl.pallas_call(store_kernel, out_shape=(jax.ShapeDtypeStruct((nb, TB, D),...  2.94 us

profile of v3, /device:TPU:0, one launch (start us, length us, event | category | flops | bytes accessed | tf_op | source)
XLA Modules:
  0.0 47.4 jit_solution(10799334648977558500)
XLA Ops:
  0.6 43.7 %xca_block.1 = (bf16[4,1024,384]{2,1,0:T(8,128)(2,1)S(1)}, bf16[4,1024,384]{2,1,0:T(8,128)(2,1)S(1)}, f32[96,1152]{1,0:T(8,128)S(1)}, f32[96,384]{1,0:T(8,128)S(...) custom-call(bf16[4,1024,384]{2,1,0:T(8,128)(2,1)} %bitcast.4, bf16[4,1024,384]{2,1,0:T(8,128)(2,1)} %bitcast.5, ...), custom_call_target="tpu_custom_call" | custom-call | tf_op jit(solution)/shard_map/xca_block/pallas_call | solution.py:403
  44.3 2.9 %xca_store.1 = (bf16[4,1024,384]{2,1,0:T(8,128)(2,1)}, bf16[4,1024,384]{2,1,0:T(8,128)(2,1)}, f32[96,1152]{1,0:T(8,128)}, f32[96,384]{1,0:T(8,128)}, f32[384]{0:T(512)}, /*index=5*/f32[384]{0:T(512)}, f32[8]{0:T(128)}) custom-call(bf16[4,1024,384]{2,1,0:T(8,128)(2,1)S(1)} %get-tuple-element.21.refs_0_, bf16[4,1024,384]{2,1,0:T(8,128)(2,1)S(1)} %get-tuple-element.22.refs_1_, ...), custom_call_target="tpu_custom_call" | custom-call | tf_op jit(solution)/shard_map/xca_store/pallas_call | solution.py:472

commit v4 on v3

--- a/solution.py
+++ b/solution.py
@@ -19,7 +19,15 @@
 OFF = 128
 ROWS = 96
 TB = 1024
-HALVES = (1, 1, 1, 2)
+PIECES = (1, 1, 1, 1)
+STEPS = {
+    (4, 3): [("b", 0, 0)],
+    (5, 2): [("b", 1, 0)],
+    (6, 2): [("c", 0, 0), ("b", 2, 0)],
+    (7, 1, 0): [("b", 3, 0), ("c", 1, 0)],
+    (7, 2, 0): [("c", 2, 0)],
+    (7, 3, 1): [("c", 3, 0)],
+}
 
 
 def mm(a, b):
@@ -102,12 +110,9 @@
         return pltpu.make_async_copy(*pairs[i], in_sem.at[i])
 
     weight_in(0).start()
-    for t in range(nb):
-        x_in(t).start()
+    x_in(0).start()
     for i in range(1, 5):
         weight_in(i).start()
-    for t in range(nb):
-        dy_in(t).start()
 
     def remote(src, dst, s, r, k):
         return pltpu.make_async_remote_copy(
@@ -122,7 +127,7 @@
         return remote(pw.at[c, rows, :], ra.at[c, xx], a_s.at[c, xx], a_r.at[c, xx], 1)
 
     def part(c, h):
-        return pl.ds(h * (ROWS // HALVES[c]), ROWS // HALVES[c])
+        return pl.ds(h * (ROWS // PIECES[c]), ROWS // PIECES[c])
 
     def stage_b(c, h):
         return remote(sa.at[c, 1 - xc, part(c, h)], rb.at[c, part(c, h)], b_s.at[c, h], b_r.at[c, h], 2)
@@ -139,21 +144,28 @@
             stage_a(c, xx).wait_recv()
             rows = pl.ds(pl.multiple_of(ROWS * (2 * xx + core), 8), ROWS)
             sa[c, xx] = pw[c, rows, :] + ra[c, xx]
-        for h in range(HALVES[c]):
+        for h in range(PIECES[c]):
             stage_b(c, h).start()
 
-    def start_c(c, h=0):
+    def start_c(c, h):
         stage_b(c, h).wait_recv()
         sb[c, part(c, h)] = sa[c, xc, part(c, h)] + rb[c, part(c, h)]
         stage_c(c, h).start()
 
-    def loop(body, steps):
-        for t in range(nb):
-            body(t)
-            if (t + 1) * 4 % nb == 0 and (t + 1) * 4 // nb - 1 in steps:
-                steps[(t + 1) * 4 // nb - 1]()
-
-    for ref in (g_lo, g_hi, sq_acc, sk_acc, gb_acc, pw):
+    def total(product):
+        out = product(0)
+        for t in range(1, nb):
+            out = out + product(t)
+        return out
+
+    def go_on(*at):
+        for stage, c, h in STEPS.get(at, ()):
+            if stage == "b":
+                start_b(c)
+            else:
+                start_c(c, h)
+
+    for ref in (g_lo, g_hi, sq_acc, sk_acc, gb_acc):
         ref[...] = jnp.zeros_like(ref)
     for i in range(3):
         weight_in(i).wait()
@@ -169,6 +181,11 @@
 
     def phase1(t):
         x_in(t).wait()
+        if t + 1 < nb:
+            x_in(t + 1).start()
+        else:
+            for n in range(nb):
+                dy_in(n).start()
         x = x_v[t].astype(F32)
         mean = jnp.mean(x, axis=-1, keepdims=True)
         cen = x - mean
@@ -190,7 +207,8 @@
         sq_acc[...] += lane_fold(qf * qf)
         sk_acc[...] += lane_fold(kf * kf)
 
-    loop(phase1, {})
+    for t in range(nb):
+        phase1(t)
 
     ex_g[0, 0:C, :] = pack(g_lo[...], g_hi[...])
     sq_row = jnp.zeros((1, D), F32)
@@ -224,7 +242,10 @@
         g_lo[...] += mm_nt(do[0:SPLIT, :], v[0:256, :])
         g_hi[...] += mm_nt(do[SPLIT:D, :], v[OFF:D, :])
 
-    loop(phase2, {0: gram_step})
+    for t in range(nb):
+        phase2(t)
+        if t == 0:
+            gram_step()
     ex_a[0] = pack(g_lo[...], g_hi[...])
     for k in range(1, 4):
         small(ex_a, exa_s, exa_r, k).start()
@@ -249,22 +270,29 @@
         o_lo, o_hi = block_mm(a_b[...], qkvt[t, 2 * D : 3 * D, :])
         ot[t, 0:SPLIT, :] = o_lo.astype(BF16)
         ot[t, SPLIT:D, :] = o_hi.astype(BF16)
-        pw[0] += mm(ot[t], dy_v[t])
-
-    loop(phase3, {})
+
+    for t in range(nb):
+        phase3(t)
+    pw[0] = total(lambda t: mm(ot[t], dy_v[t]))
     start_a(0)
 
     def phase4(t):
         dv_lo, dv_hi = block_mm(a_bt[...], dot_v[t])
         qkvt[t, 2 * D : 2 * D + SPLIT, :] = dv_lo.astype(BF16)
         qkvt[t, 2 * D + SPLIT : 3 * D, :] = dv_hi.astype(BF16)
-        pw[1] += mm_nt(ut[t], qkvt[t, 2 * D : 3 * D, :])
-
-    loop(phase4, {1: lambda: start_b(0)})
+
+    for t in range(nb):
+        phase4(t)
+    go_on(4, 0)
+    pw[1, :, 0:256] = total(lambda t: mm_nt(ut[t], qkvt[t, 2 * D : 2 * D + 256, :]))
+    go_on(4, 1)
+    pw[1, :, 256:D] = total(lambda t: mm_nt(ut[t], qkvt[t, 2 * D + 256 : 3 * D, :]))
+    go_on(4, 2)
     start_a(1)
 
     for k in range(1, 4):
         small(ex_a, exa_s, exa_r, k).wait_recv()
+    go_on(4, 3)
     d_attn = (ex_a[0] + ex_a[1]) + (ex_a[2] + ex_a[3])
     drk = jnp.zeros((1, D), F32)
     lane = lax.broadcasted_iota(jnp.int32, (8, 128), 1)
@@ -298,9 +326,14 @@
         ds = dsq_v[:, 0:1]
         dot_v[t, 0:SPLIT, :] = (dq_lo + ds[0:SPLIT] * qf[0:SPLIT]).astype(BF16)
         dot_v[t, SPLIT:D, :] = (dq_hi + ds[SPLIT:D] * qf[SPLIT:D]).astype(BF16)
-        pw[2] += mm_nt(ut[t], dot_v[t])
-
-    loop(phase5, {0: lambda: start_b(1), 3: lambda: start_c(0)})
+
+    for t in range(nb):
+        phase5(t)
+    go_on(5, 0)
+    pw[2, :, 0:256] = total(lambda t: mm_nt(ut[t], dot_v[t, 0:256, :]))
+    go_on(5, 1)
+    pw[2, :, 256:D] = total(lambda t: mm_nt(ut[t], dot_v[t, 256:D, :]))
+    go_on(5, 2)
     start_a(2)
 
     def phase6(t):
@@ -309,32 +342,34 @@
         ds = dsk_v[:, 0:1]
         qkvt[t, D : D + SPLIT, :] = (dk_lo + ds[0:SPLIT] * kf[0:SPLIT]).astype(BF16)
         qkvt[t, D + SPLIT : 2 * D, :] = (dk_hi + ds[SPLIT:D] * kf[SPLIT:D]).astype(BF16)
-        pw[3] += mm_nt(ut[t], qkvt[t, D : 2 * D, :])
-
-    loop(phase6, {1: lambda: start_b(2), 2: lambda: start_c(1)})
+
+    for t in range(nb):
+        phase6(t)
+    go_on(6, 0)
+    pw[3, :, 0:256] = total(lambda t: mm_nt(ut[t], qkvt[t, D : D + 256, :]))
+    go_on(6, 1)
+    pw[3, :, 256:D] = total(lambda t: mm_nt(ut[t], qkvt[t, D + 256 : 2 * D, :]))
+    go_on(6, 2)
     start_a(3)
 
-    def phase7(t):
-        du_t = mm(wqkv_ref[:, 0:D], dot_v[t]) + mm(wqkv_ref[:, D : 3 * D], qkvt[t, D : 3 * D, :])
+    def phase7(t, half):
+        rows = slice(half * (TB // 2), (half + 1) * (TB // 2))
+        du_t = mm(wqkv_ref[:, 0:D], dot_v[t, :, rows]) + mm(wqkv_ref[:, D : 3 * D], qkvt[t, D : 3 * D, rows])
         du = du_t.astype(BF16).T.astype(F32)
-        rstd = rstd_v[t][:, 0:1]
-        xhat = (x_v[t].astype(F32) - mean_v[t][:, 0:1]) * rstd
+        rstd = rstd_v[t, rows, 0:1]
+        xhat = (x_v[t, rows].astype(F32) - mean_v[t, rows, 0:1]) * rstd
         g = du * gamma
         m1 = jnp.mean(g, axis=-1, keepdims=True)
         m2 = jnp.mean(g * xhat, axis=-1, keepdims=True)
         dx = rstd * (g - m1 - xhat * m2)
-        dx_v[t] = (dy_v[t].astype(F32) + dx).astype(BF16)
-        gb_acc[0] += jnp.sum((du * xhat).reshape(TB // 8, 8, D), axis=0)
-        gb_acc[1] += jnp.sum(du.reshape(TB // 8, 8, D), axis=0)
-
-    loop(
-        phase7,
-        {
-            0: lambda: start_b(3),
-            1: lambda: start_c(2),
-            2: lambda: start_c(3, 0),
-            3: lambda: start_c(3, 1),
-        })
+        dx_v[t, rows] = (dy_v[t, rows].astype(F32) + dx).astype(BF16)
+        gb_acc[0] += jnp.sum((du * xhat).reshape(TB // 16, 8, D), axis=0)
+        gb_acc[1] += jnp.sum(du.reshape(TB // 16, 8, D), axis=0)
+
+    for t in range(nb):
+        for half in range(2):
+            phase7(t, half)
+            go_on(7, t, half)
 
     dgam = jnp.sum(gb_acc[0], axis=0, keepdims=True)
     dbet = jnp.sum(gb_acc[1], axis=0, keepdims=True)
@@ -345,17 +380,19 @@
     def phase8(t):
         y_v[t] = (x_v[t].astype(F32) + mm(ot[t].T, wo_ref[...])).astype(BF16)
 
-    loop(phase8, {})
+    for t in range(nb):
+        phase8(t)
+        go_on(8, t, 1)
 
     for c in range(4):
-        for h in range(HALVES[c]):
+        for h in range(PIECES[c]):
             stage_c(c, h).wait_recv()
-        total = sb[c] + rc[c]
+        both = sb[c] + rc[c]
         if c == 0:
-            gwo_ref[...] = total
+            gwo_ref[...] = both
         else:
             col = {1: 2 * D, 2: 0, 3: D}[c]
-            gwqkv_ref[:, col : col + D] = total
+            gwqkv_ref[:, col : col + D] = both
     t_copy.wait_recv()
     gtau_ref[...] = (ex_t[0] + ex_t[1])[0, 0:H]
     for k in range(1, 8):
@@ -369,7 +406,7 @@
     for c in range(4):
         for xx in range(2):
             stage_a(c, xx).wait_send()
-        for h in range(HALVES[c]):
+        for h in range(PIECES[c]):
             stage_b(c, h).wait_send()
             stage_c(c, h).wait_send()
     g_core.wait_send()
@@ -381,7 +418,12 @@
 
 def store_kernel(*refs):
     sem = refs[14]
-    copies = [pltpu.make_async_copy(refs[i], refs[7 + i], sem.at[i]) for i in range(7)]
+    copies = []
+    for i in range(7):
+        src, dst = refs[i], refs[7 + i]
+        for at in range(src.shape[0]) if i < 2 else [None]:
+            pair = (src, dst) if at is None else (src.at[at], dst.at[at])
+            copies.append(pltpu.make_async_copy(*pair, sem.at[len(copies)]))
     for copy in copies:
         copy.start()
     for copy in copies:
@@ -453,7 +495,7 @@
                 pltpu.VMEM((2, 8, 128), F32),
                 dma((nb,)), dma((nb,)), dma((5,)),
                 dma((2,)), dma((2,)), dma((4,)), dma((4,)),
-                dma((4, 2)), dma((4, 2)), dma((4, 2)), dma((4, 2)), dma((4, 2)), dma((4, 2)),
+                dma((4, 2)), dma((4, 2)), dma((4, max(PIECES))), dma((4, max(PIECES))), dma((4, max(PIECES))), dma((4, max(PIECES))),
                 dma((8,)), dma((8,)), dma, dma,
             ],
             compiler_params=pltpu.CompilerParams(
@@ -482,7 +524,7 @@
             ),
             in_specs=[hbm] * 7,
             out_specs=(hbm,) * 7,
-            scratch_shapes=[dma((7,))],
+            scratch_shapes=[dma((2 * nb + 5,))],
             compiler_params=pltpu.CompilerParams(vmem_limit_bytes=4 * 2**20),
             name="xca_store",
         )(*outs)

time: 47.5 us -> 46.6 us (0.981)
  Pallas kernels: 46.6 us -> 45.7 us
    pallas_call x1, Pallas kernels: 43.7 us -> 42.8 us  [local_block(): pl.pallas_call(functools.partial(kernel, nb), out_shape=(pltpu.VMEM((nb,...]
where the time goes in v4:
time: 46.6 us; the launch traced here: 46.5 us
  Pallas kernels  45.7 us (98%)
  between operations  0.8 us (2%)
    pallas_call x1, Pallas kernels, local_block(): pl.pallas_call(functools.partial(kernel, nb), out_shape=(pltpu.VMEM((nb,...  42.8 us
    pallas_call x1, Pallas kernels, local_block(): pl.pallas_call(store_kernel, out_shape=(jax.ShapeDtypeStruct((nb, TB, D),...  2.94 us

profile of v4, /device:TPU:0, one launch (start us, length us, event | category | flops | bytes accessed | tf_op | source)
XLA Modules:
  0.0 46.5 jit_solution(13869306454809191156)
XLA Ops:
  0.6 42.8 %xca_block.1 = (bf16[4,1024,384]{2,1,0:T(8,128)(2,1)S(1)}, bf16[4,1024,384]{2,1,0:T(8,128)(2,1)S(1)}, f32[96,1152]{1,0:T(8,128)S(1)}, f32[96,384]{1,0:T(8,128)S(...) custom-call(bf16[4,1024,384]{2,1,0:T(8,128)(2,1)} %bitcast.4, bf16[4,1024,384]{2,1,0:T(8,128)(2,1)} %bitcast.5, ...), custom_call_target="tpu_custom_call" | custom-call | tf_op jit(solution)/shard_map/xca_block/pallas_call | solution.py:445
  43.4 2.9 %xca_store.1 = (bf16[4,1024,384]{2,1,0:T(8,128)(2,1)}, bf16[4,1024,384]{2,1,0:T(8,128)(2,1)}, f32[96,1152]{1,0:T(8,128)}, f32[96,384]{1,0:T(8,128)}, f32[384]{0:T(512)}, /*index=5*/f32[384]{0:T(512)}, f32[8]{0:T(128)}) custom-call(bf16[4,1024,384]{2,1,0:T(8,128)(2,1)S(1)} %get-tuple-element.21.refs_0_, bf16[4,1024,384]{2,1,0:T(8,128)(2,1)S(1)} %get-tuple-element.22.refs_1_, ...), custom_call_target="tpu_custom_call" | custom-call | tf_op jit(solution)/shard_map/xca_store/pallas_call | solution.py:514

commit v5 on v4

--- a/solution.py
+++ b/solution.py
@@ -19,14 +19,14 @@
 OFF = 128
 ROWS = 96
 TB = 1024
-PIECES = (1, 1, 1, 1)
+PIECES = (2, 1, 1, 2)
 STEPS = {
     (4, 3): [("b", 0, 0)],
-    (5, 2): [("b", 1, 0)],
-    (6, 2): [("c", 0, 0), ("b", 2, 0)],
-    (7, 1, 0): [("b", 3, 0), ("c", 1, 0)],
-    (7, 2, 0): [("c", 2, 0)],
-    (7, 3, 1): [("c", 3, 0)],
+    (5, 2): [("b", 1, 0), ("c", 0, 0)],
+    (6, 2): [("b", 2, 0), ("c", 0, 1)],
+    (7, 0, 1): [("b", 3, 0), ("c", 1, 0)],
+    (7, 2, 1): [("c", 2, 0)],
+    (7, 3, 1): [("c", 3, 0), ("c", 3, 1)],
 }
 
 
@@ -170,6 +170,9 @@
     for i in range(3):
         weight_in(i).wait()
     wqkvt[...] = wqkv_ref[...].T
+    x_in(0).wait()
+    for t in range(1, nb):
+        x_in(t).start()
     gamma = gamma_ref[...].reshape(1, D)
     beta = beta_ref[...].reshape(1, D)
 
@@ -180,12 +183,6 @@
         return out
 
     def phase1(t):
-        x_in(t).wait()
-        if t + 1 < nb:
-            x_in(t + 1).start()
-        else:
-            for n in range(nb):
-                dy_in(n).start()
         x = x_v[t].astype(F32)
         mean = jnp.mean(x, axis=-1, keepdims=True)
         cen = x - mean
@@ -208,6 +205,13 @@
         sk_acc[...] += lane_fold(kf * kf)
 
     for t in range(nb):
+        if t == 1:
+            for n in range(1, nb):
+                x_in(n).wait()
+            for n in range(nb):
+                dy_in(n).start()
+            for i in range(3, 5):
+                weight_in(i).wait()
         phase1(t)
 
     ex_g[0, 0:C, :] = pack(g_lo[...], g_hi[...])
@@ -222,8 +226,8 @@
     g_core = remote(ex_g.at[0], ex_g.at[1], exg_s.at[0], exg_r.at[0], 1)
     g_chip = remote(ex_h.at[0], ex_h.at[1], exg_s.at[1], exg_r.at[1], 2)
     g_core.start()
-    for i in range(3, 5):
-        weight_in(i).wait()
+    for t in range(nb):
+        dy_in(t).wait()
 
     def gram_step():
         g_core.wait_recv()
@@ -234,7 +238,6 @@
     g_hi[...] = jnp.zeros_like(g_hi)
 
     def phase2(t):
-        dy_in(t).wait()
         v = mm(wqkvt[2 * D : 3 * D, :], ut[t]).astype(BF16)
         qkvt[t, 2 * D : 3 * D, :] = v
         do = mm_nt(wo_ref[...], dy_v[t]).astype(BF16)

time: 46.6 us -> 46.2 us (level)
  Pallas kernels: 45.7 us -> 45.2 us
    pallas_call x1, Pallas kernels: 42.8 us -> 42.3 us  [local_block(): pl.pallas_call(functools.partial(kernel, nb), out_shape=(pltpu.VMEM((nb,...]
where the time goes in v5:
time: 46.2 us; the launch traced here: 46 us
  Pallas kernels  45.2 us (98%)
  between operations  0.8 us (2%)
    pallas_call x1, Pallas kernels, local_block(): pl.pallas_call(functools.partial(kernel, nb), out_shape=(pltpu.VMEM((nb,...  42.3 us
    pallas_call x1, Pallas kernels, local_block(): pl.pallas_call(store_kernel, out_shape=(jax.ShapeDtypeStruct((nb, TB, D),...  2.94 us

profile of v5, /device:TPU:0, one launch (start us, length us, event | category | flops | bytes accessed | tf_op | source)
XLA Modules:
  0.0 46.0 jit_solution(9942475836969380912)
XLA Ops:
  0.6 42.3 %xca_block.1 = (bf16[4,1024,384]{2,1,0:T(8,128)(2,1)S(1)}, bf16[4,1024,384]{2,1,0:T(8,128)(2,1)S(1)}, f32[96,1152]{1,0:T(8,128)S(1)}, f32[96,384]{1,0:T(8,128)S(...) custom-call(bf16[4,1024,384]{2,1,0:T(8,128)(2,1)} %bitcast.4, bf16[4,1024,384]{2,1,0:T(8,128)(2,1)} %bitcast.5, ...), custom_call_target="tpu_custom_call" | custom-call | tf_op jit(solution)/shard_map/xca_block/pallas_call | solution.py:448
  42.9 2.9 %xca_store.1 = (bf16[4,1024,384]{2,1,0:T(8,128)(2,1)}, bf16[4,1024,384]{2,1,0:T(8,128)(2,1)}, f32[96,1152]{1,0:T(8,128)}, f32[96,384]{1,0:T(8,128)}, f32[384]{0:T(512)}, /*index=5*/f32[384]{0:T(512)}, f32[8]{0:T(128)}) custom-call(bf16[4,1024,384]{2,1,0:T(8,128)(2,1)S(1)} %get-tuple-element.21.refs_0_, bf16[4,1024,384]{2,1,0:T(8,128)(2,1)S(1)} %get-tuple-element.22.refs_1_, ...), custom_call_target="tpu_custom_call" | custom-call | tf_op jit(solution)/shard_map/xca_store/pallas_call | solution.py:517

commit v6 on v5

--- a/solution.py
+++ b/solution.py
@@ -19,11 +19,11 @@
 OFF = 128
 ROWS = 96
 TB = 1024
-PIECES = (2, 1, 1, 2)
+PIECES = (3, 1, 1, 2)
 STEPS = {
     (4, 3): [("b", 0, 0)],
     (5, 2): [("b", 1, 0), ("c", 0, 0)],
-    (6, 2): [("b", 2, 0), ("c", 0, 1)],
+    (6, 2): [("b", 2, 0), ("c", 0, 1), ("c", 0, 2)],
     (7, 0, 1): [("b", 3, 0), ("c", 1, 0)],
     (7, 2, 1): [("c", 2, 0)],
     (7, 3, 1): [("c", 3, 0), ("c", 3, 1)],

time: 46.2 us -> 45.9 us (level)
  no operation moved by 1% of the time
where the time goes in v6:
time: 45.9 us; the launch traced here: 45.8 us
  Pallas kernels  45 us (98%)
  between operations  0.8 us (2%)
    pallas_call x1, Pallas kernels, local_block(): pl.pallas_call(functools.partial(kernel, nb), out_shape=(pltpu.VMEM((nb,...  42 us
    pallas_call x1, Pallas kernels, local_block(): pl.pallas_call(store_kernel, out_shape=(jax.ShapeDtypeStruct((nb, TB, D),...  2.94 us

profile of v6, /device:TPU:0, one launch (start us, length us, event | category | flops | bytes accessed | tf_op | source)
XLA Modules:
  0.0 45.8 jit_solution(13535629720083196465)
XLA Ops:
  0.6 42.0 %xca_block.1 = (bf16[4,1024,384]{2,1,0:T(8,128)(2,1)S(1)}, bf16[4,1024,384]{2,1,0:T(8,128)(2,1)S(1)}, f32[96,1152]{1,0:T(8,128)S(1)}, f32[96,384]{1,0:T(8,128)S(...) custom-call(bf16[4,1024,384]{2,1,0:T(8,128)(2,1)} %bitcast.4, bf16[4,1024,384]{2,1,0:T(8,128)(2,1)} %bitcast.5, ...), custom_call_target="tpu_custom_call" | custom-call | tf_op jit(solution)/shard_map/xca_block/pallas_call | solution.py:448
  42.7 2.9 %xca_store.1 = (bf16[4,1024,384]{2,1,0:T(8,128)(2,1)}, bf16[4,1024,384]{2,1,0:T(8,128)(2,1)}, f32[96,1152]{1,0:T(8,128)}, f32[96,384]{1,0:T(8,128)}, f32[384]{0:T(512)}, /*index=5*/f32[384]{0:T(512)}, f32[8]{0:T(128)}) custom-call(bf16[4,1024,384]{2,1,0:T(8,128)(2,1)S(1)} %get-tuple-element.21.refs_0_, bf16[4,1024,384]{2,1,0:T(8,128)(2,1)S(1)} %get-tuple-element.22.refs_1_, ...), custom_call_target="tpu_custom_call" | custom-call | tf_op jit(solution)/shard_map/xca_store/pallas_call | solution.py:517
